TPU v7x, 128 devices: a whole 4x4x4 slice. The times are simulated.
128 devices in a mesh: dp: 8 (over x, y_lo), vocab: 16 (over z, y_hi, core).
Axes of the slice: x: 4, y: 4 (y_hi: 2, y_lo: 2; y = y_hi * 2 + y_lo), z: 4, core: 2. Of those that a mesh axis runs over, the one named last changes fastest.
Arguments:
- hidden: bfloat16 [8192, 5120], P(('dp', 'vocab')), may hold values from -100 to 100
- tokens: int32 [8192], P('dp'), may hold values from 0 to 18431
- old_weight: bfloat16 [18432, 5120], P('vocab'), may hold values from -1 to 1
- new_weight: bfloat16 [18432, 5120], P('dp', 'vocab'), may hold values from -6 to 6
Outputs:
- logprob: float32 [8192], P(('dp', 'vocab'))
- engine_weight: bfloat16 [18432, 5120], P('vocab')
All inputs are finite; a program needn't handle non-finite values.
Results may differ from a plain program's by a relative error of at most 0.001.
Values may be sent and summed in bfloat16 or wider, within the bound.
No kernel may reach another device: no remote copies, remote signals or barrier semaphores. Data moves between devices by JAX's collectives and lax.ppermute only.
A program may use at most 128 MiB of HBM per device.

v0:
```python
import jax
import jax.numpy as jnp
from jax import lax
from jax.sharding import Mesh
from jax.sharding import PartitionSpec as P

DP = ("dp_0", "dp_1")
DP_VOCAB = ("dp_0", "dp_1", "vocab")


def sent_together(arrays, axis, split_dim, concat_dim, along):
    ends, at = ([], 0)
    for a in arrays[:-1]:
        at += a.shape[along]
        ends.append(at)
    both = jnp.concatenate(arrays, axis=along)
    return tuple(
        jnp.split(
            lax.all_to_all(both, axis, split_axis=split_dim, concat_axis=concat_dim, tiled=True),
            ends,
            axis=along,
        )
    )


def whole_of(shard, axes, dim):
    if not axes:
        return shard
    nearer = lax.all_gather(shard, axes[-1], axis=dim, tiled=True)
    return whole_of(nearer, axes[:-1], dim)


def on_device(hidden, tokens, old_weight, new_weight):
    ranks = lax.axis_size("vocab")
    rank = lax.axis_index("vocab")
    vocab_rows = old_weight.shape[0]
    first_id = rank * vocab_rows
    own_rows = hidden.shape[0]
    logits = lax.dot_general(
        lax.all_gather(hidden, "vocab", axis=0, tiled=True),
        old_weight,
        (((1,), (1,)), ((), ())),
        preferred_element_type=jnp.float32,
    )
    highest = jnp.max(logits, axis=1)
    summed = jnp.sum(jnp.exp(logits - highest[:, None]), axis=1)
    wanted = tokens - first_id
    columns = lax.broadcasted_iota(jnp.int32, logits.shape, 1)
    target = jnp.sum(jnp.where(columns == wanted[:, None], logits, 0.0), axis=1)
    stats = jnp.stack([highest, summed, target], axis=0)
    highest, summed, target = (stats[0], stats[1], stats[2])
    shaped = (
        highest.reshape(ranks, own_rows),
        summed.reshape(ranks, own_rows),
        target.reshape(ranks, own_rows),
    )
    got_high, got_sum, got_target = sent_together(
        (shaped[0], shaped[1], shaped[2]), "vocab", 0, 0, 1
    )
    highest = jnp.max(got_high, axis=0)
    summed = jnp.sum(got_sum * jnp.exp(got_high - highest[None, :]), axis=0)
    target = jnp.sum(got_target, axis=0)
    logprob = target - highest - jnp.log(summed)
    replicas = lax.axis_size(DP)
    trainer_cols = new_weight.shape[1]
    owned = lax.all_to_all(
        lax.all_to_all(new_weight, DP, split_axis=1, concat_axis=0, tiled=True),
        "vocab",
        split_axis=0,
        concat_axis=1,
        tiled=True,
    )
    owner_count = owned.shape[0]
    shaped_pieces = owned.reshape(owner_count, ranks, 1, trainer_cols // replicas)
    complete = whole_of(shaped_pieces, DP, 2)
    engine_weight = complete.reshape(owner_count, ranks * trainer_cols)
    return (logprob, engine_weight)


def solution(mesh):
    finer = Mesh(mesh.devices.reshape(4, 2, mesh.shape["vocab"]), ("dp_0", "dp_1", "vocab"))
    return jax.shard_map(
        on_device,
        mesh=finer,
        in_specs=(P(DP_VOCAB, None), P(DP), P("vocab", None), P(DP, "vocab")),
        out_specs=(P(DP_VOCAB), P("vocab", None)),
        check_vma=False,
    )
```

profile of v0, /device:TPU:1, one launch (start us, length us, event | category | flops | bytes accessed | tf_op | source)
XLA Modules:
  0.0 325.5 jit_solution(2934551947676968886)
XLA Ops:
  7.2 0.0 all-gather.9.cloned.1.call-start
  7.2 24.7 %all_to_all.44 = bf16[2304,8,40]{0,2,1:T(8,128)(2,1)S(1)} all-to-all(bf16[2304,8,40]{0,2,1:T(8,128)(2,1)} %bitcast.16), channel_id=1, replica_groups=mesh['dp_0'=4,'dp_1'=2,'vocab'=16] {'dp_0','dp_1'}, dimensions={1} | all-to-all | bytes 2949120 | tf_op jit(solution)/shard_map/all_to_all | solution.py:67
  31.9 0.2 copy.9
  32.2 0.5 all_to_all.38
  32.7 0.3 copy.10
  33.0 31.0 %all_to_all.45 = bf16[16,1152,40]{1,2,0:T(8,128)(2,1)S(1)} all-to-all(bf16[16,1152,40]{1,2,0:T(8,128)(2,1)S(1)} %copy.10), channel_id=1, replica_groups=mesh['dp_0'=4,'dp_1'=2,'vocab'=16] {'vocab'}, dimensions={0} | all-to-all | bytes 2949120 | tf_op jit(solution)/shard_map/all_to_all | solution.py:66
  64.0 1.3 copy.11
  65.3 0.0 all-gather.5.cloned.1.call-start
  65.3 0.7 all-gather.5.cloned.1.call-update
  66.0 0.0 all-gather.7.cloned.1.call-start
  66.1 40.3 %all-gather.9.cloned.1.call-done = bf16[1152,16,80]{0,1,2:T(8,128)(2,1)} async-done(((bf16[1152,16,40]{0,1,2:T(8,128)(2,1)}), bf16[1152,16,80]{0,1,2:T(8,128)(2,1)}) %all-gather.9.cloned.1.call-update) | async-done | bytes 2949136 | tf_op jit(solution)/shard_map/all_gather | solution.py:29
  106.3 4.0 %copy.12 = bf16[1152,16,80]{0,2,1:T(8,128)(2,1)} copy(bf16[1152,16,80]{0,1,2:T(8,128)(2,1)} %all-gather.9.cloned.1.call-done) | data formatting | bytes 5898240 | tf_op jit(solution)/shard_map/all_gather | solution.py:29
  110.4 81.7 %all-gather.5.cloned.1.call-done = bf16[1024,5120]{1,0:T(8,128)(2,1)} async-done(((bf16[64,5120]{1,0:T(8,128)(2,1)}), bf16[1024,5120]{1,0:T(8,128)(2,1)}) %all-gather.5.cloned.1.call-update) | async-done | bytes 10485776 | tf_op jit(solution)/shard_map/all_gather | solution.py:40
  192.1 19.5 %fusion.1 = (f32[1024]{0:T(1024)S(1)}, f32[1024,1152]{1,0:T(8,128)}) fusion(bf16[1024,5120]{1,0:T(8,128)(2,1)} %all-gather.5.cloned.1.call-done, bf16[1152,5120]{1,0:T(8,128)(2,1)} %param.6), kind=kOutput, calls=%fused_computation.11 | convolution fusion | flops 12080774144 | bytes 27004928 | tf_op jit(solution)/shard_map/dot_general | solution.py:39
  211.5 0.1 reshape_squeeze_stack.9
  211.6 3.1 exponential_reduce_fusion
  214.8 0.1 reshape_squeeze_stack.10
  214.8 0.1 reshape_squeeze_stack.11
  214.9 0.1 pad_maximum_fusion
  215.0 10.4 %all_to_all.46 = f32[16,1,192]{2,1,0:T(1,128)S(1)} all-to-all(f32[16,1,192]{2,1,0:T(1,128)S(1)} %all_to_all.32), channel_id=1, replica_groups=mesh['dp_0'=4,'dp_1'=2,'vocab'=16] {'vocab'}, dimensions={0} | all-to-all | bytes 24576 | tf_op jit(solution)/shard_map/all_to_all | solution.py:19
  225.4 0.1 slice_reduce_fusion
  225.5 0.5 log_subtract_fusion
  226.0 76.7 %all-gather.7.cloned.1.call-done = bf16[1152,16,8,40]{0,3,2,1:T(8,128)(2,1)} async-done(((bf16[1152,16,2,40]{0,3,2,1:T(8,128)(2,1)}), bf16[1152,16,8,40]{0,3,2,1:T(8,128)(2,1)}) %all-gather.7.cloned.1.call-update) | async-done | bytes 11796496 | tf_op jit(solution)/shard_map/all_gather | solution.py:29
  302.7 16.3 %copy.13 = bf16[1152,5120]{1,0:T(8,128)(2,1)} copy(bf16[1152,5120]{0,1:T(8,128)(2,1)} %bitcast.12) | data formatting | bytes 23592960
  (8 shorter events, 0.1 us)
Async XLA Ops:
  7.2 99.1 %all-gather.9.cloned.1.call-start = ((), (), s32[]{:S(2)}) async-start(), calls=%async_computation.5 | async-start | bytes 4423680 | tf_op jit(solution)/shard_map/all_gather | solution.py:29
  65.2 45.1 %copy-start = (s32[1024]{0:T(1024)S(1)}, s32[1024]{0:T(1024)}, u32[]{:S(2)}) copy-start(s32[1024]{0:T(1024)} %param.5) | copy-start | bytes 12292
  65.3 126.8 %all-gather.5.cloned.1.call-start = ((), (), s32[]{:S(2)}) async-start(), calls=%async_computation.3 | async-start | bytes 11141120 | tf_op jit(solution)/shard_map/all_gather | solution.py:40
  66.0 236.7 %all-gather.7.cloned.1.call-start = ((), (), s32[]{:S(2)}) async-start(), calls=%async_computation.4 | async-start | bytes 14745600 | tf_op jit(solution)/shard_map/all_gather | solution.py:29
Sparse Core Ops, SparseCore 0:
  65.4 40.8 all-gather.8
  108.8 83.2 all-gather.4
  193.7 108.8 all-gather.6
where the time goes:
time: 326 us; the launch traced here: 325 us
  waiting for transfers between devices  199 us (61%)
  blocking collectives  66 us (20%)
  local copies, waits for them, and re-layouts  22.8 us (7%)
  matrix products  19.5 us (6%)
  between operations  13.8 us (4%)
  other arithmetic  3.87 us (1%)
    all_gather x2, waiting for transfers between devices, whole_of(): nearer = lax.all_gather(shard, axes[-1], axis=dim, tiled=True)  117 us
    all_gather x1, waiting for transfers between devices, on_device(): lax.all_gather(hidden, 'vocab', axis=0, tiled=True)  81.7 us
    all_to_all x1, blocking collectives, on_device(): lax.all_to_all(lax.all_to_all(new_weight, DP, split_axis=1, concat_axis=0...  31 us
    all_to_all x1, blocking collectives, on_device(): lax.all_to_all(new_weight, DP, split_axis=1, concat_axis=0, tiled=True)  24.7 us
    dot_general x1, matrix products, on_device(): lax.dot_general(lax.all_gather(hidden, 'vocab', axis=0, tiled=True), old_...  19.5 us
    unnamed x4, local copies, waits for them, and re-layouts  16.3 us
    all_to_all x1, blocking collectives, sent_together(): lax.all_to_all(both, axis, split_axis=split_dim, concat_axis=concat_dim,...  10.4 us
  transfers between devices with their start and end apart: 3, of which 3 were waited for; matrix products, arithmetic and copies ran while one was open for 8% of the time, Pallas kernels for 0%

commit v1 on v0

v1 whole, which is shorter than its diff:
```python
import jax
import jax.numpy as jnp
from jax import lax
from jax.experimental import pallas as pl
from jax.experimental.pallas import tpu as pltpu
from jax.sharding import Mesh
from jax.sharding import PartitionSpec as P

AXES = ("x", "q", "z", "h", "k")
SIZES = (4, 2, 4, 2, 2)
CHUNK = 288
ROWS_A = 176


def place(x, q, z, h, k):
    return (((x * 2 + q) * 4 + z) * 2 + h) * 2 + k


def pairs(move):
    found = []
    for x in range(4):
        for q in range(2):
            for z in range(4):
                for h in range(2):
                    for k in range(2):
                        found.append((place(x, q, z, h, k), place(*move(x, q, z, h, k))))
    return found


def send(value, move):
    return lax.ppermute(value, AXES, pairs(move))


def swap_core(value):
    return send(value, lambda x, q, z, h, k: (x, q, z, h, 1 - k))


def swap_q(value):
    return send(value, lambda x, q, z, h, k: (x, 1 - q, z, h, k))


def swap_h(value):
    return send(value, lambda x, q, z, h, k: (x, q, z, 1 - h, k))


def along_z(value, step):
    return send(value, lambda x, q, z, h, k: (x, q, (z + step) % 4, h, k))


def along_x(value, step):
    return send(value, lambda x, q, z, h, k: ((x + step) % 4, q, z, h, k))


def to_owner(value, step):
    return send(value, lambda x, q, z, h, k: ((z + step) % 4, (h + step // 2) % 2, x, q, k))


def turn_kernel(where_ref, own_ref, got_ref, *refs):
    outs, scratch = refs[:4], refs[4]
    own, got = own_ref[...], got_ref[...]
    first = where_ref[0] == 0
    both = jnp.concatenate([jnp.where(first, own, got), jnp.where(first, got, own)], axis=0)
    scratch[...] = both.T
    for step in range(4):
        start = pl.multiple_of(((where_ref[1] + step) % 4) * CHUNK, 32)
        outs[step][...] = scratch[pl.ds(start, CHUNK), :]


def turn(where, turned, got):
    width, rows = got.shape
    return pl.pallas_call(
        turn_kernel,
        out_shape=[jax.ShapeDtypeStruct((CHUNK, 2 * width), got.dtype)] * 4,
        grid_spec=pltpu.PrefetchScalarGridSpec(
            num_scalar_prefetch=1,
            grid=(1,),
            in_specs=[
                pl.BlockSpec((width, rows), lambda i, where: (0, where[0])),
                pl.BlockSpec((width, rows), lambda i, where: (0, 0)),
            ],
            out_specs=[pl.BlockSpec((CHUNK, 2 * width), lambda i, where: (0, 0))] * 4,
            scratch_shapes=[pltpu.VMEM((rows, 2 * width), got.dtype)],
        ),
        name="turn",
    )(where, turned, got)


def laid(spots):
    def kernel(where_ref, *refs):
        count = len(spots)
        blocks, stages = refs[:count], refs[-count - 2 : -2]
        out_ref, into, out_of = refs[-count - 3], refs[-2], refs[-1]
        loads = [
            pltpu.make_async_copy(block, stage, into.at[i]) for i, (block, stage) in enumerate(zip(blocks, stages))
        ]
        for load in loads:
            load.start()
        stores = []
        for load, stage, (dx, other, steps, first) in zip(loads, stages, spots):
            load.wait()
            source = (where_ref[0] + dx) % 4
            rows = stage.shape[1]
            for at, step in enumerate(steps):
                h = (where_ref[1] + other + step // 2) % 2
                column = ((source - step + 4) % 4 * 2 + h) * 640
                row = source * CHUNK + first
                store = pltpu.make_async_copy(
                    stage.at[at],
                    out_ref.at[pl.ds(pl.multiple_of(row, 16), rows), pl.ds(pl.multiple_of(column, 128), 640)],
                    out_of.at[len(stores)],
                )
                store.start()
                stores.append(store)
        for store in stores:
            store.wait()

    return kernel


def lay(where, blocks, spots, into=None):
    count = sum(len(spot[2]) for spot in spots)
    anywhere = pl.BlockSpec(memory_space=pl.ANY)
    operands = list(blocks) + ([] if into is None else [into])
    return pl.pallas_call(
        laid(spots),
        out_shape=jax.ShapeDtypeStruct((4 * CHUNK, 5120), blocks[0].dtype),
        grid_spec=pltpu.PrefetchScalarGridSpec(
            num_scalar_prefetch=1,
            grid=(1,),
            in_specs=[anywhere] * len(operands),
            out_specs=anywhere,
            scratch_shapes=[pltpu.VMEM(block.shape, block.dtype) for block in blocks]
            + [pltpu.SemaphoreType.DMA((len(blocks),)), pltpu.SemaphoreType.DMA((count,))],
        ),
        input_output_aliases={} if into is None else {len(operands): 0},
        name="lay",
    )(where, *operands)


def first_moves(new_weight):
    rows = new_weight.shape[0] // 2
    z, core = lax.axis_index("z"), lax.axis_index("k")
    turned = new_weight.T
    other = lax.dynamic_slice(turned, (0, (1 - core) * rows), (turned.shape[0], rows))
    chunks = turn(jnp.stack([core, z]).astype(jnp.int32), turned, swap_core(other))
    got = [to_owner(chunks[step], step) for step in range(4)]
    own_a = jnp.stack([block[:ROWS_A] for block in got])
    own_b = jnp.stack([block[ROWS_A:] for block in got])
    return own_a, own_b


def move_weight(own_a, own_b):
    x, q = lax.axis_index("x"), lax.axis_index("q")
    ya = swap_q(own_a)
    a_m, a_p = along_x(own_a, 1), along_x(own_a, -1)
    yb = swap_q(own_b)
    b_m, b_p = along_x(own_b, 1), along_x(own_b, -1)
    a_2 = along_x(a_m, 1)
    b_2 = along_x(b_p, -1)
    ya_m, ya_p = along_x(ya, 1), along_x(ya, -1)
    ya_2 = along_x(ya_p, -1)
    yb_m = swap_q(b_m)
    yb_p = swap_q(b_p)
    yb_2 = swap_q(b_2)
    four = (0, 1, 2, 3)
    where = jnp.stack([x, q]).astype(jnp.int32)
    out = lay(
        where,
        [own_a, own_b, a_m, a_p, b_m, b_p, ya, yb],
        [
            (0, 0, four, 0),
            (0, 0, four, ROWS_A),
            (3, 0, four, 0),
            (1, 0, four, 0),
            (3, 0, four, ROWS_A),
            (1, 0, four, ROWS_A),
            (0, 1, four, 0),
            (0, 1, four, ROWS_A),
        ],
    )
    return lay(
        where,
        [a_2, b_2, ya_m, ya_p, yb_m, yb_p, ya_2, yb_2],
        [
            (2, 0, four, 0),
            (2, 0, four, ROWS_A),
            (3, 1, four, 0),
            (1, 1, four, 0),
            (3, 1, four, ROWS_A),
            (1, 1, four, ROWS_A),
            (2, 1, four, 0),
            (2, 1, four, ROWS_A),
        ],
        out,
    )


def stats_kernel(ids_ref, near_ref, far_ref, weight_ref, out_ref, rows_ref, sems):
    step = pl.program_id(0)
    half = near_ref.shape[0]

    @pl.when(step == 0)
    def _():
        copies = [
            pltpu.make_async_copy(near_ref, rows_ref.at[pl.ds(0, half)], sems.at[0]),
            pltpu.make_async_copy(far_ref, rows_ref.at[pl.ds(half, half)], sems.at[1]),
        ]
        for copy in copies:
            copy.start()
        for copy in copies:
            copy.wait()

    logits = lax.dot_general(
        weight_ref[...], rows_ref[...], (((1,), (1,)), ((), ())), preferred_element_type=jnp.float32
    )
    ids = lax.broadcasted_iota(jnp.int32, logits.shape, 0) + step * logits.shape[0]
    found = jnp.sum(jnp.where(ids == ids_ref[...], logits, 0.0), axis=0, keepdims=True)
    top = jnp.max(logits, axis=0, keepdims=True)

    @pl.when(step == 0)
    def _():
        out_ref[0:1] = top
        out_ref[1:2] = jnp.sum(jnp.exp(logits - top), axis=0, keepdims=True)
        out_ref[2:3] = found

    @pl.when(step > 0)
    def _():
        before = out_ref[0:1]
        highest = jnp.maximum(before, top)
        summed = jnp.sum(jnp.exp(logits - highest), axis=0, keepdims=True)
        out_ref[0:1] = highest
        out_ref[1:2] = out_ref[1:2] * jnp.exp(before - highest) + summed
        out_ref[2:3] = out_ref[2:3] + found


def part_stats(near, far, weight, ids):
    count = 2 * near.shape[0]
    tile = 384
    anywhere = pl.BlockSpec(memory_space=pl.ANY)
    return pl.pallas_call(
        stats_kernel,
        out_shape=jax.ShapeDtypeStruct((3, count), jnp.float32),
        grid=(weight.shape[0] // tile,),
        in_specs=[
            pl.BlockSpec((1, count), lambda i: (0, 0)),
            anywhere,
            anywhere,
            pl.BlockSpec((tile, weight.shape[1]), lambda i: (i, 0)),
        ],
        out_specs=pl.BlockSpec((3, count), lambda i: (0, 0)),
        scratch_shapes=[pltpu.VMEM((count, weight.shape[1]), near.dtype), pltpu.SemaphoreType.DMA((2,))],
        name="stats",
    )(ids.reshape(1, count), near, far, weight)


def by_owner(stats):
    z, h, k = lax.axis_index("z"), lax.axis_index("h"), lax.axis_index("k")
    stats = stats[::-1]
    stats = jnp.concatenate([stats, stats], axis=0)
    stats = lax.dynamic_slice_in_dim(stats, (3 - z) % 4, 4, axis=0)
    stats = jnp.where(h == 0, stats, stats[:, ::-1])
    return jnp.where(k == 0, stats, stats[:, :, ::-1])


def relative(owned):
    z, h, k = lax.axis_index("z"), lax.axis_index("h"), lax.axis_index("k")
    owned = jnp.where(k == 0, owned, owned[:, :, ::-1])
    owned = jnp.where(h == 0, owned, owned[:, ::-1])
    owned = owned[::-1]
    owned = jnp.concatenate([owned, owned], axis=0)
    return lax.dynamic_slice_in_dim(owned, (3 - z) % 4, 4, axis=0)


def log_probs(hidden, tokens, old_weight):
    own_rows = hidden.shape[0]
    rank = (lax.axis_index("z") * 2 + lax.axis_index("h")) * 2 + lax.axis_index("k")
    wanted = relative(tokens.reshape(4, 2, 2, own_rows)) - rank * old_weight.shape[0]
    m, p = along_z(hidden, 1), along_z(hidden, -1)
    flipped = swap_h(hidden)
    far = along_z(m, 1)
    groups = [jnp.concatenate([hidden, m, far, p], axis=0)]
    m, p = along_z(flipped, 1), along_z(flipped, -1)
    far = along_z(p, -1)
    groups.append(jnp.concatenate([flipped, m, far, p], axis=0))
    stats = []
    for flip, group in enumerate(groups):
        ids = wanted[:, flip].transpose(1, 0, 2).reshape(-1)
        stats.append(part_stats(group, swap_core(group), old_weight, ids).reshape(3, 2, 4, own_rows))
    stats = jnp.stack(stats, axis=0).transpose(3, 0, 2, 1, 4)
    stats = by_owner(stats).reshape(16, 3 * own_rows)
    stats = lax.all_to_all(stats, ("z", "h", "k"), split_axis=0, concat_axis=0, tiled=True)
    stats = stats.reshape(16, 3, own_rows)
    highest = jnp.max(stats[:, 0], axis=0)
    summed = jnp.sum(stats[:, 1] * jnp.exp(stats[:, 0] - highest[None, :]), axis=0)
    target = jnp.sum(stats[:, 2], axis=0)
    return target - highest - jnp.log(summed)


def on_device(hidden, tokens, old_weight, new_weight):
    own_a, own_b = first_moves(new_weight)
    return log_probs(hidden, tokens, old_weight), move_weight(own_a, own_b)


def solution(mesh):
    finer = Mesh(mesh.devices.reshape(SIZES), AXES)
    return jax.shard_map(
        on_device,
        mesh=finer,
        in_specs=(P(AXES, None), P(("x", "q")), P(("z", "h", "k"), None), P(("x", "q"), ("z", "h", "k"))),
        out_specs=(P(AXES), P(("z", "h", "k"), None)),
        check_vma=False,
    )
```

time: 326 us -> 235 us (0.72)
  waiting for transfers between devices: 199 us -> 87.1 us
  starting transfers between devices: 0.12 us -> 82.3 us
  blocking collectives: 66 us -> 0 us
  Pallas kernels: 0 us -> 41.1 us
  matrix products: 19.5 us -> 0 us
  between operations: 13.8 us -> 1 us
  local copies, waits for them, and re-layouts: 22.8 us -> 18 us
    all_gather x3 -> x0, waiting for transfers between devices: 199 us -> none  [the longest x2 117 us: whole_of(): nearer = lax.all_gather(shard, axes[-1], axis=dim, tiled=True)]
    ppermute x0 -> x28, waiting for transfers between devices: none -> 86.4 us  [send(): return lax.ppermute(value, AXES, pairs(move))]
    ppermute x0 -> x28, starting transfers between devices: none -> 71.7 us  [send(): return lax.ppermute(value, AXES, pairs(move))]
    all_to_all x3 -> x0, blocking collectives: 66 us -> none  [the longest x1 31 us: on_device(): lax.all_to_all(lax.all_to_all(new_weight, DP, split_axis=1, concat_axis=0...]
    pallas_call x0 -> x5, Pallas kernels: none -> 41.1 us  [the longest x2 25.7 us: part_stats(): pl.pallas_call(stats_kernel, out_shape=jax.ShapeDtypeStruct((3, count), j...]
    dot_general x1 -> x0, matrix products: 19.5 us -> none  [on_device(): lax.dot_general(lax.all_gather(hidden, 'vocab', axis=0, tiled=True), old_...]
    all_to_all x0 -> x1, starting transfers between devices: none -> 10.6 us  [log_probs(): lax.all_to_all(stats, ('z', 'h', 'k'), split_axis=0, concat_axis=0, tiled...]
    unnamed x4 -> x28, local copies, waits for them, and re-layouts: 16.3 us -> 8.85 us
  transfers between devices with their start and end apart: 3 -> 29, of which waited for: 3 -> 10; matrix products, arithmetic and copies ran while one was open for 8% -> 7% of each run, Pallas kernels for 0% -> 18%
where the time goes in v1:
time: 235 us; the launch traced here: 232 us
  waiting for transfers between devices  87.1 us (37%)
  starting transfers between devices  82.3 us (35%)
  Pallas kernels  41.1 us (17%)
  local copies, waits for them, and re-layouts  18 us (8%)
    ppermute x28, waiting for transfers between devices, send(): return lax.ppermute(value, AXES, pairs(move))  86.4 us
    ppermute x28, starting transfers between devices, send(): return lax.ppermute(value, AXES, pairs(move))  71.7 us
    pallas_call x2, Pallas kernels, part_stats(): pl.pallas_call(stats_kernel, out_shape=jax.ShapeDtypeStruct((3, count), j...  25.7 us
    pallas_call x2, Pallas kernels, lay(): pl.pallas_call(laid(spots), out_shape=jax.ShapeDtypeStruct((4 * CHUNK, 51...  11.8 us
    all_to_all x1, starting transfers between devices, log_probs(): lax.all_to_all(stats, ('z', 'h', 'k'), split_axis=0, concat_axis=0, tiled...  10.6 us
    unnamed x28, local copies, waits for them, and re-layouts  8.85 us
  transfers between devices with their start and end apart: 29, of which 10 were waited for; matrix products, arithmetic and copies ran while one was open for 7% of the time, Pallas kernels for 18%

profile of v1, /device:TPU:1, one launch (start us, length us, event | category | flops | bytes accessed | tf_op | source)
XLA Modules:
  0.0 231.7 jit_solution(10039697199251825467)
XLA Ops:
  0.6 4.6 %collective-permute-start.2 = (bf16[64,5120]{1,0:T(8,128)(2,1)}, bf16[64,5120]{1,0:T(8,128)(2,1)}, u32[]{:S(2)}, u32[]{:S(2)}) collective-permute-start(bf16[64,5120]{1,0:T(8,128)(2,1)} %param.4), channel_id=1, source_target_pairs={{0,12},{1,13},{2,14},{3,15},{4,0},{5,1},{6,2},{7,3},{8,4},{9,5},{1... | collective-permute-start | bytes 1966088 | tf_op jit(solution)/shard_map/ppermute | solution.py:31
  5.3 2.9 %collective-permute-start.4 = (bf16[64,5120]{1,0:T(8,128)(2,1)}, bf16[64,5120]{1,0:T(8,128)(2,1)}, u32[]{:S(2)}, u32[]{:S(2)}) collective-permute-start(bf16[64,5120]{1,0:T(8,128)(2,1)} %param.4), channel_id=1, source_target_pairs={{0,2},{1,3},{2,0},{3,1},{4,6},{5,7},{6,4},{7,5},{8,10},{9,11},{10,... | collective-permute-start | bytes 1966088 | tf_op jit(solution)/shard_map/ppermute | solution.py:31
  8.2 2.0 dynamic-slice_bitcast_fusion
  14.0 8.1 %collective-permute-done = bf16[64,5120]{1,0:T(8,128)(2,1)} collective-permute-done((bf16[64,5120]{1,0:T(8,128)(2,1)}, bf16[64,5120]{1,0:T(8,128)(2,1)}, u32[]{:S(2)}, u32[]{:S(2)}) %collective-permute-start) | collective-permute-done | bytes 655392 | tf_op jit(solution)/shard_map/ppermute | solution.py:31
  22.5 2.4 %collective-permute-start.6 = (bf16[64,5120]{1,0:T(8,128)(2,1)}, bf16[64,5120]{1,0:T(8,128)(2,1)}, u32[]{:S(2)}, u32[]{:S(2)}) collective-permute-start(bf16[64,5120]{1,0:T(8,128)(2,1)} %collective-permute-done.4), channel_id=1, source_target_pairs={{0,12},{1,13},{2,14},{3,15},{4,0},{5,1},{6,2},{7,3},{8,4},{9,5},{1... | collective-permute-start | bytes 1966088 | tf_op jit(solution)/shard_map/ppermute | solution.py:31
  26.9 3.6 %turn.1 = (bf16[288,640]{1,0:T(8,128)(2,1)}, bf16[288,640]{1,0:T(8,128)(2,1)}, bf16[288,640]{1,0:T(8,128)(2,1)}, bf16[288,640]{1,0:T(8,128)(2,1)}) custom-call(s32[2]{0:T(128)} %pad_add_fusion.1.where_ref, bf16[320,2304]{1,0:T(8,128)(2,1)} %bitcast.37, bf16[320,1152]{1,0:T(8,128)(2,1)} %copy-done.3), custom_call_target="tpu_custom_call" | custom-call | tf_op jit(solution)/shard_map/turn/pallas_call | solution.py:71
  35.7 23.7 %collective-permute-start.12 = (bf16[288,640]{1,0:T(8,128)(2,1)}, bf16[288,640]{1,0:T(8,128)(2,1)S(1)}, u32[]{:S(2)}, u32[]{:S(2)}) collective-permute-start(bf16[288,640]{1,0:T(8,128)(2,1)} %get-tuple-element.8), channel_id=1, source_target_pairs={{0,80},{1,81},{2,64},{3,65},{4,112},{5,113},{6,96},{7,97},{8,16},{... | collective-permute-start | bytes 1105928 | tf_op jit(solution)/shard_map/ppermute | solution.py:31
  59.4 10.3 %collective-permute-start.13 = (bf16[288,640]{1,0:T(8,128)(2,1)}, bf16[288,640]{1,0:T(8,128)(2,1)S(1)}, u32[]{:S(2)}, u32[]{:S(2)}) collective-permute-start(bf16[288,640]{1,0:T(8,128)(2,1)} %get-tuple-element.9), channel_id=1, source_target_pairs={{0,112},{1,113},{2,96},{3,97},{4,16},{5,17},{6,0},{7,1},{8,48},{9,... | collective-permute-start | bytes 1105928 | tf_op jit(solution)/shard_map/ppermute | solution.py:31
  69.7 15.4 %collective-permute-done.12 = bf16[288,640]{1,0:T(8,128)(2,1)S(1)} collective-permute-done((bf16[288,640]{1,0:T(8,128)(2,1)}, bf16[288,640]{1,0:T(8,128)(2,1)S(1)}, u32[]{:S(2)}, u32[]{:S(2)}) %collective-permute-start.12) | collective-permute-done | bytes 368672 | tf_op jit(solution)/shard_map/ppermute | solution.py:31
  85.1 12.2 %collective-permute-done.13 = bf16[288,640]{1,0:T(8,128)(2,1)S(1)} collective-permute-done((bf16[288,640]{1,0:T(8,128)(2,1)}, bf16[288,640]{1,0:T(8,128)(2,1)S(1)}, u32[]{:S(2)}, u32[]{:S(2)}) %collective-permute-start.13) | collective-permute-done | bytes 368672 | tf_op jit(solution)/shard_map/ppermute | solution.py:31
  97.4 3.4 %collective-permute-start.27 = (bf16[4,112,640]{2,1,0:T(8,128)(2,1)S(1)}, bf16[4,112,640]{2,1,0:T(8,128)(2,1)S(1)}, u32[]{:S(2)}, u32[]{:S(2)}) collective-permute-start(bf16[4,112,640]{2,1,0:T(8,128)(2,1)S(1)} %pad_maximum_fusion.1.refs_1_), channel_id=1, source_target_pairs={{0,16},{1,17},{2,18},{3,19},{4,20},{5,21},{6,22},{7,23},{8,24},{9,... | collective-permute-start | bytes 1720328 | tf_op jit(solution)/shard_map/ppermute | solution.py:31
  103.0 2.7 %collective-permute-start.16 = (bf16[4,112,640]{2,1,0:T(8,128)(2,1)S(1)}, bf16[4,112,640]{2,1,0:T(8,128)(2,1)S(1)}, u32[]{:S(2)}, u32[]{:S(2)}) collective-permute-start(bf16[4,112,640]{2,1,0:T(8,128)(2,1)S(1)} %pad_maximum_fusion.1.refs_1_), channel_id=1, source_target_pairs={{0,96},{1,97},{2,98},{3,99},{4,100},{5,101},{6,102},{7,103},{8,104... | collective-permute-start | bytes 1720328 | tf_op jit(solution)/shard_map/ppermute | solution.py:31
  105.6 3.3 %collective-permute-start.7 = (bf16[64,5120]{1,0:T(8,128)(2,1)}, bf16[64,5120]{1,0:T(8,128)(2,1)S(1)}, u32[]{:S(2)}, u32[]{:S(2)}) collective-permute-start(bf16[64,5120]{1,0:T(8,128)(2,1)} %collective-permute-done.6), channel_id=1, source_target_pairs={{0,12},{1,13},{2,14},{3,15},{4,0},{5,1},{6,2},{7,3},{8,4},{9,5},{1... | collective-permute-start | bytes 1966088 | tf_op jit(solution)/shard_map/ppermute | solution.py:31
  109.0 2.0 constant_dynamic-update-slice_fusion.near_ref
  112.1 10.5 %collective-permute-done.7 = bf16[64,5120]{1,0:T(8,128)(2,1)S(1)} collective-permute-done((bf16[64,5120]{1,0:T(8,128)(2,1)}, bf16[64,5120]{1,0:T(8,128)(2,1)S(1)}, u32[]{:S(2)}, u32[]{:S(2)}) %collective-permute-start.7) | collective-permute-done | bytes 655392 | tf_op jit(solution)/shard_map/ppermute | solution.py:31
  128.8 18.7 %collective-permute-done.18.refs_6_ = bf16[4,176,640]{2,1,0:T(8,128)(2,1)} collective-permute-done((bf16[4,176,640]{2,1,0:T(8,128)(2,1)S(1)}, bf16[4,176,640]{2,1,0:T(8,128)(2,1)}, u32[]{:S(2)}, u32[]{:S(2)}) %collective-permute-start.18) | collective-permute-done | bytes 901152 | tf_op jit(solution)/shard_map/ppermute | solution.py:31
  151.5 17.0 %collective-permute-done.20.refs_3_ = bf16[4,176,640]{2,1,0:T(8,128)(2,1)} collective-permute-done((bf16[4,176,640]{2,1,0:T(8,128)(2,1)}, bf16[4,176,640]{2,1,0:T(8,128)(2,1)}, u32[]{:S(2)}, u32[]{:S(2)}) %collective-permute-start.20) | collective-permute-done | bytes 901152 | tf_op jit(solution)/shard_map/ppermute | solution.py:31
  169.5 2.0 collective-permute-start.24
  172.9 12.8 %stats.2 = f32[3,512]{1,0:T(4,128)} custom-call(s32[1,512]{1,0:T(1,128)} %reshape_reshape.6.ids_ref, bf16[256,5120]{1,0:T(8,128)(2,1)} %constant_dynamic-update-slice_fusion.near_ref, bf16[256,5120]{1,0:T(8,128)(2,1)} %collective-permute-done.3.far_ref, bf16[1152,5120]{1,0:T(8,128)(2,1)} %weight_ref.3), custom_call_target="tpu_custom_call" | custom-call | tf_op jit(solution)/shard_map/stats/pallas_call | solution.py:240
  186.5 12.9 %stats.3 = f32[3,512]{1,0:T(4,128)} custom-call(s32[1,512]{1,0:T(1,128)} %reshape_reshape.7.ids_ref, bf16[256,5120]{1,0:T(8,128)(2,1)} %copy-done, bf16[256,5120]{1,0:T(8,128)(2,1)} %collective-permute-done.8.far_ref, bf16[1152,5120]{1,0:T(8,128)(2,1)} %weight_ref.3), custom_call_target="tpu_custom_call" | custom-call | tf_op jit(solution)/shard_map/stats/pallas_call | solution.py:240
  202.6 10.6 %all-to-all-start = ((f32[16,1,192]{2,1,0:T(1,128)}), f32[16,1,192]{2,1,0:T(1,128)S(1)}, u32[]{:S(2)}, u32[]{:S(2)}) async-start(f32[16,1,192]{2,1,0:T(1,128)} %all_to_all.8), calls=%async_computation | async-start | bytes 32768 | tf_op jit(solution)/shard_map/all_to_all | solution.py:291
  213.9 5.9 %lay.2.refs_8_ = bf16[1152,5120]{1,0:T(8,128)(2,1)} custom-call(s32[2]{0:T(128)} %pad_add_fusion.where_ref, bf16[4,176,640]{2,1,0:T(8,128)(2,1)} %copy-done.1, bf16[4,112,640]{2,1,0:T(8,128)(2,1)} %copy-done.2, bf16[4,176,640]{2,1,0:T(8,128)(2,1)} %collective-permute-done.14.refs_2_, bf16[4,176,640]{2,1,0:T(8,128)(2,1)} %collective-permute-done.26.refs_3_, ...), custom_call_target="tpu_custom_call" | custom-call | tf_op jit(solution)/shard_map/lay/pallas_call | solution.py:124
  219.8 3.7 %collective-permute-done.25.refs_7_ = bf16[4,112,640]{2,1,0:T(8,128)(2,1)S(1)} collective-permute-done((bf16[4,112,640]{2,1,0:T(8,128)(2,1)}, bf16[4,112,640]{2,1,0:T(8,128)(2,1)S(1)}, u32[]{:S(2)}, u32[]{:S(2)}) %collective-permute-start.25) | collective-permute-done | bytes 573472 | tf_op jit(solution)/shard_map/ppermute | solution.py:31
  224.3 5.9 %lay.3 = bf16[1152,5120]{1,0:T(8,128)(2,1)} custom-call(s32[2]{0:T(128)} %pad_add_fusion.where_ref, bf16[4,176,640]{2,1,0:T(8,128)(2,1)} %collective-permute-done.15.refs_0_, bf16[4,112,640]{2,1,0:T(8,128)(2,1)} %collective-permute-done.17.refs_1_, bf16[4,176,640]{2,1,0:T(8,128)(2,1)} %collective-permute-done.19.refs_2_, ...), custom_call_target="tpu_custom_call", output_to_operand_aliasing={{}: (9, {})} | custom-call | tf_op jit(solution)/shard_map/lay/pallas_call | solution.py:124
  (109 shorter events, 33.9 us)
Async XLA Ops:
  0.6 102.3 %collective-permute-start.2 = (bf16[64,5120]{1,0:T(8,128)(2,1)}, bf16[64,5120]{1,0:T(8,128)(2,1)}, u32[]{:S(2)}, u32[]{:S(2)}) collective-permute-start(bf16[64,5120]{1,0:T(8,128)(2,1)} %param.4), channel_id=1, source_target_pairs={{0,12},{1,13},{2,14},{3,15},{4,0},{5,1},{6,2},{7,3},{8,4},{9,5},{1... | collective-permute-start | bytes 1966088 | tf_op jit(solution)/shard_map/ppermute | solution.py:31
  22.1 78.8 %collective-permute-start.1 = (bf16[64,5120]{1,0:T(8,128)(2,1)}, bf16[64,5120]{1,0:T(8,128)(2,1)}, u32[]{:S(2)}, u32[]{:S(2)}) collective-permute-start(bf16[64,5120]{1,0:T(8,128)(2,1)} %collective-permute-done), channel_id=1, source_target_pairs={{0,4},{1,5},{2,6},{3,7},{4,8},{5,9},{6,10},{7,11},{8,12},{9,13},{1... | collective-permute-start | bytes 1966088 | tf_op jit(solution)/shard_map/ppermute | solution.py:31
  22.5 83.2 %collective-permute-start.6 = (bf16[64,5120]{1,0:T(8,128)(2,1)}, bf16[64,5120]{1,0:T(8,128)(2,1)}, u32[]{:S(2)}, u32[]{:S(2)}) collective-permute-start(bf16[64,5120]{1,0:T(8,128)(2,1)} %collective-permute-done.4), channel_id=1, source_target_pairs={{0,12},{1,13},{2,14},{3,15},{4,0},{5,1},{6,2},{7,3},{8,4},{9,5},{1... | collective-permute-start | bytes 1966088 | tf_op jit(solution)/shard_map/ppermute | solution.py:31
  32.1 27.2 %collective-permute-start.11 = (bf16[288,640]{1,0:T(8,128)(2,1)}, bf16[288,640]{1,0:T(8,128)(2,1)S(1)}, u32[]{:S(2)}, u32[]{:S(2)}) collective-permute-start(bf16[288,640]{1,0:T(8,128)(2,1)} %get-tuple-element.7), channel_id=1, source_target_pairs={{0,32},{1,33},{2,48},{3,49},{4,64},{5,65},{6,80},{7,81},{8,96},{9,... | collective-permute-start | bytes 1105928 | tf_op jit(solution)/shard_map/ppermute | solution.py:31
  35.7 49.4 %collective-permute-start.12 = (bf16[288,640]{1,0:T(8,128)(2,1)}, bf16[288,640]{1,0:T(8,128)(2,1)S(1)}, u32[]{:S(2)}, u32[]{:S(2)}) collective-permute-start(bf16[288,640]{1,0:T(8,128)(2,1)} %get-tuple-element.8), channel_id=1, source_target_pairs={{0,80},{1,81},{2,64},{3,65},{4,112},{5,113},{6,96},{7,97},{8,16},{... | collective-permute-start | bytes 1105928 | tf_op jit(solution)/shard_map/ppermute | solution.py:31
  59.4 37.9 %collective-permute-start.13 = (bf16[288,640]{1,0:T(8,128)(2,1)}, bf16[288,640]{1,0:T(8,128)(2,1)S(1)}, u32[]{:S(2)}, u32[]{:S(2)}) collective-permute-start(bf16[288,640]{1,0:T(8,128)(2,1)} %get-tuple-element.9), channel_id=1, source_target_pairs={{0,112},{1,113},{2,96},{3,97},{4,16},{5,17},{6,0},{7,1},{8,48},{9,... | collective-permute-start | bytes 1105928 | tf_op jit(solution)/shard_map/ppermute | solution.py:31
  85.1 25.9 %collective-permute-start.5 = (bf16[64,5120]{1,0:T(8,128)(2,1)}, bf16[64,5120]{1,0:T(8,128)(2,1)S(1)}, u32[]{:S(2)}, u32[]{:S(2)}) collective-permute-start(bf16[64,5120]{1,0:T(8,128)(2,1)} %collective-permute-done.4), channel_id=1, source_target_pairs={{0,4},{1,5},{2,6},{3,7},{4,8},{5,9},{6,10},{7,11},{8,12},{9,13},{1... | collective-permute-start | bytes 1966088 | tf_op jit(solution)/shard_map/ppermute | solution.py:31
  97.4 28.3 %collective-permute-start.27 = (bf16[4,112,640]{2,1,0:T(8,128)(2,1)S(1)}, bf16[4,112,640]{2,1,0:T(8,128)(2,1)S(1)}, u32[]{:S(2)}, u32[]{:S(2)}) collective-permute-start(bf16[4,112,640]{2,1,0:T(8,128)(2,1)S(1)} %pad_maximum_fusion.1.refs_1_), channel_id=1, source_target_pairs={{0,16},{1,17},{2,18},{3,19},{4,20},{5,21},{6,22},{7,23},{8,24},{9,... | collective-permute-start | bytes 1720328 | tf_op jit(solution)/shard_map/ppermute | solution.py:31
  100.9 26.4 %collective-permute-start.21 = (bf16[4,112,640]{2,1,0:T(8,128)(2,1)S(1)}, bf16[4,112,640]{2,1,0:T(8,128)(2,1)S(1)}, u32[]{:S(2)}, u32[]{:S(2)}) collective-permute-start(bf16[4,112,640]{2,1,0:T(8,128)(2,1)S(1)} %pad_maximum_fusion.1.refs_1_), channel_id=1, source_target_pairs={{0,32},{1,33},{2,34},{3,35},{4,36},{5,37},{6,38},{7,39},{8,40},{9,... | collective-permute-start | bytes 1720328 | tf_op jit(solution)/shard_map/ppermute | solution.py:31
  103.0 25.8 %collective-permute-start.16 = (bf16[4,112,640]{2,1,0:T(8,128)(2,1)S(1)}, bf16[4,112,640]{2,1,0:T(8,128)(2,1)S(1)}, u32[]{:S(2)}, u32[]{:S(2)}) collective-permute-start(bf16[4,112,640]{2,1,0:T(8,128)(2,1)S(1)} %pad_maximum_fusion.1.refs_1_), channel_id=1, source_target_pairs={{0,96},{1,97},{2,98},{3,99},{4,100},{5,101},{6,102},{7,103},{8,104... | collective-permute-start | bytes 1720328 | tf_op jit(solution)/shard_map/ppermute | solution.py:31
  111.0 57.6 %collective-permute-start.3 = (bf16[256,5120]{1,0:T(8,128)(2,1)}, bf16[256,5120]{1,0:T(8,128)(2,1)}, u32[]{:S(2)}, u32[]{:S(2)}) collective-permute-start(bf16[256,5120]{1,0:T(8,128)(2,1)} %constant_dynamic-update-slice_fusion.near_ref), channel_id=1, source_target_pairs={{0,1},{1,0},{2,3},{3,2},{4,5},{5,4},{6,7},{7,6},{8,9},{9,8},{10,11... | collective-permute-start | bytes 7864328 | tf_op jit(solution)/shard_map/ppermute | solution.py:31
  123.8 45.7 %collective-permute-start.8 = (bf16[256,5120]{1,0:T(8,128)(2,1)S(1)}, bf16[256,5120]{1,0:T(8,128)(2,1)}, u32[]{:S(2)}, u32[]{:S(2)}) collective-permute-start(bf16[256,5120]{1,0:T(8,128)(2,1)S(1)} %constant_dynamic-update-slice_fusion.4.near_ref), channel_id=1, source_target_pairs={{0,1},{1,0},{2,3},{3,2},{4,5},{5,4},{6,7},{7,6},{8,9},{9,8},{10,11... | collective-permute-start | bytes 7864328 | tf_op jit(solution)/shard_map/ppermute | solution.py:31
  125.8 21.7 %collective-permute-start.18 = (bf16[4,176,640]{2,1,0:T(8,128)(2,1)S(1)}, bf16[4,176,640]{2,1,0:T(8,128)(2,1)}, u32[]{:S(2)}, u32[]{:S(2)}) collective-permute-start(bf16[4,176,640]{2,1,0:T(8,128)(2,1)S(1)} %pad_maximum_fusion.refs_0_), channel_id=1, source_target_pairs={{0,16},{1,17},{2,18},{3,19},{4,20},{5,21},{6,22},{7,23},{8,24},{9,... | collective-permute-start | bytes 2703368 | tf_op jit(solution)/shard_map/ppermute | solution.py:31
  127.3 21.8 %collective-permute-start.26 = (bf16[4,176,640]{2,1,0:T(8,128)(2,1)S(1)}, bf16[4,176,640]{2,1,0:T(8,128)(2,1)}, u32[]{:S(2)}, u32[]{:S(2)}) collective-permute-start(bf16[4,176,640]{2,1,0:T(8,128)(2,1)S(1)} %pad_maximum_fusion.refs_0_), channel_id=1, source_target_pairs={{0,96},{1,97},{2,98},{3,99},{4,100},{5,101},{6,102},{7,103},{8,104... | collective-permute-start | bytes 2703368 | tf_op jit(solution)/shard_map/ppermute | solution.py:31
  128.7 22.3 %collective-permute-start.14 = (bf16[4,176,640]{2,1,0:T(8,128)(2,1)S(1)}, bf16[4,176,640]{2,1,0:T(8,128)(2,1)}, u32[]{:S(2)}, u32[]{:S(2)}) collective-permute-start(bf16[4,176,640]{2,1,0:T(8,128)(2,1)S(1)} %pad_maximum_fusion.refs_0_), channel_id=1, source_target_pairs={{0,32},{1,33},{2,34},{3,35},{4,36},{5,37},{6,38},{7,39},{8,40},{9,... | collective-permute-start | bytes 2703368 | tf_op jit(solution)/shard_map/ppermute | solution.py:31
  147.5 21.1 %collective-permute-start.20 = (bf16[4,176,640]{2,1,0:T(8,128)(2,1)}, bf16[4,176,640]{2,1,0:T(8,128)(2,1)}, u32[]{:S(2)}, u32[]{:S(2)}) collective-permute-start(bf16[4,176,640]{2,1,0:T(8,128)(2,1)} %collective-permute-done.18.refs_6_), channel_id=1, source_target_pairs={{0,96},{1,97},{2,98},{3,99},{4,100},{5,101},{6,102},{7,103},{8,104... | collective-permute-start | bytes 2703368 | tf_op jit(solution)/shard_map/ppermute | solution.py:31
  149.1 51.1 %collective-permute-start.22 = (bf16[4,112,640]{2,1,0:T(8,128)(2,1)}, bf16[4,112,640]{2,1,0:T(8,128)(2,1)}, u32[]{:S(2)}, u32[]{:S(2)}) collective-permute-start(bf16[4,112,640]{2,1,0:T(8,128)(2,1)} %copy-done.5), channel_id=1, source_target_pairs={{0,16},{1,17},{2,18},{3,19},{4,20},{5,21},{6,22},{7,23},{8,24},{9,... | collective-permute-start | bytes 1720328 | tf_op jit(solution)/shard_map/ppermute | solution.py:31
  151.0 50.7 %collective-permute-start.17 = (bf16[4,112,640]{2,1,0:T(8,128)(2,1)}, bf16[4,112,640]{2,1,0:T(8,128)(2,1)}, u32[]{:S(2)}, u32[]{:S(2)}) collective-permute-start(bf16[4,112,640]{2,1,0:T(8,128)(2,1)} %copy-done.6), channel_id=1, source_target_pairs={{0,96},{1,97},{2,98},{3,99},{4,100},{5,101},{6,102},{7,103},{8,104... | collective-permute-start | bytes 1720328 | tf_op jit(solution)/shard_map/ppermute | solution.py:31
  168.6 55.0 %collective-permute-start.19 = (bf16[4,176,640]{2,1,0:T(8,128)(2,1)}, bf16[4,176,640]{2,1,0:T(8,128)(2,1)}, u32[]{:S(2)}, u32[]{:S(2)}) collective-permute-start(bf16[4,176,640]{2,1,0:T(8,128)(2,1)} %collective-permute-done.18.refs_6_), channel_id=1, source_target_pairs={{0,32},{1,33},{2,34},{3,35},{4,36},{5,37},{6,38},{7,39},{8,40},{9,... | collective-permute-start | bytes 2703368 | tf_op jit(solution)/shard_map/ppermute | solution.py:31
  168.6 54.9 %collective-permute-start.15 = (bf16[4,176,640]{2,1,0:T(8,128)(2,1)}, bf16[4,176,640]{2,1,0:T(8,128)(2,1)}, u32[]{:S(2)}, u32[]{:S(2)}) collective-permute-start(bf16[4,176,640]{2,1,0:T(8,128)(2,1)} %collective-permute-done.14.refs_2_), channel_id=1, source_target_pairs={{0,32},{1,33},{2,34},{3,35},{4,36},{5,37},{6,38},{7,39},{8,40},{9,... | collective-permute-start | bytes 2703368 | tf_op jit(solution)/shard_map/ppermute | solution.py:31
  169.5 54.0 %collective-permute-start.24 = (bf16[4,176,640]{2,1,0:T(8,128)(2,1)}, bf16[4,176,640]{2,1,0:T(8,128)(2,1)}, u32[]{:S(2)}, u32[]{:S(2)}) collective-permute-start(bf16[4,176,640]{2,1,0:T(8,128)(2,1)} %collective-permute-done.20.refs_3_), channel_id=1, source_target_pairs={{0,96},{1,97},{2,98},{3,99},{4,100},{5,101},{6,102},{7,103},{8,104... | collective-permute-start | bytes 2703368 | tf_op jit(solution)/shard_map/ppermute | solution.py:31
  200.2 19.6 %collective-permute-start.23 = (bf16[4,112,640]{2,1,0:T(8,128)(2,1)S(1)}, bf16[4,112,640]{2,1,0:T(8,128)(2,1)S(1)}, u32[]{:S(2)}, u32[]{:S(2)}) collective-permute-start(bf16[4,112,640]{2,1,0:T(8,128)(2,1)S(1)} %copy-done.7), channel_id=1, source_target_pairs={{0,16},{1,17},{2,18},{3,19},{4,20},{5,21},{6,22},{7,23},{8,24},{9,... | collective-permute-start | bytes 1720328 | tf_op jit(solution)/shard_map/ppermute | solution.py:31
  201.8 21.8 %collective-permute-start.25 = (bf16[4,112,640]{2,1,0:T(8,128)(2,1)}, bf16[4,112,640]{2,1,0:T(8,128)(2,1)S(1)}, u32[]{:S(2)}, u32[]{:S(2)}) collective-permute-start(bf16[4,112,640]{2,1,0:T(8,128)(2,1)} %collective-permute-done.17.refs_1_), channel_id=1, source_target_pairs={{0,16},{1,17},{2,18},{3,19},{4,20},{5,21},{6,22},{7,23},{8,24},{9,... | collective-permute-start | bytes 1720328 | tf_op jit(solution)/shard_map/ppermute | solution.py:31
  202.6 28.3 %all-to-all-start = ((f32[16,1,192]{2,1,0:T(1,128)}), f32[16,1,192]{2,1,0:T(1,128)S(1)}, u32[]{:S(2)}, u32[]{:S(2)}) async-start(f32[16,1,192]{2,1,0:T(1,128)} %all_to_all.8), calls=%async_computation | async-start | bytes 32768 | tf_op jit(solution)/shard_map/all_to_all | solution.py:291
  (16 other events, 335.8 us)

commit v2 on v1

--- a/solution.py
+++ b/solution.py
@@ -8,8 +8,10 @@
 
 AXES = ("x", "q", "z", "h", "k")
 SIZES = (4, 2, 4, 2, 2)
+TILE = 384
+TILE = 384
+STATS_VMEM = 56
 CHUNK = 288
-ROWS_A = 176
 
 
 def place(x, q, z, h, k):
@@ -52,7 +54,7 @@
 
 
 def to_owner(value, step):
-    return send(value, lambda x, q, z, h, k: ((z + step) % 4, (h + step // 2) % 2, x, q, k))
+    return send(value, lambda x, q, z, h, k: ((x + z + step) % 4, h, x, q, k))
 
 
 def turn_kernel(where_ref, own_ref, got_ref, *refs):
@@ -81,6 +83,7 @@
             out_specs=[pl.BlockSpec((CHUNK, 2 * width), lambda i, where: (0, 0))] * 4,
             scratch_shapes=[pltpu.VMEM((rows, 2 * width), got.dtype)],
         ),
+        compiler_params=pltpu.CompilerParams(vmem_limit_bytes=16 << 20),
         name="turn",
     )(where, turned, got)
 
@@ -96,17 +99,16 @@
         for load in loads:
             load.start()
         stores = []
-        for load, stage, (dx, other, steps, first) in zip(loads, stages, spots):
+        for load, stage, (dx, other, steps) in zip(loads, stages, spots):
             load.wait()
             source = (where_ref[0] + dx) % 4
-            rows = stage.shape[1]
             for at, step in enumerate(steps):
-                h = (where_ref[1] + other + step // 2) % 2
-                column = ((source - step + 4) % 4 * 2 + h) * 640
-                row = source * CHUNK + first
+                h = (where_ref[1] + other) % 2
+                column = ((source - where_ref[2] - step + 8) % 4 * 2 + h) * 640
+                row = source * CHUNK
                 store = pltpu.make_async_copy(
                     stage.at[at],
-                    out_ref.at[pl.ds(pl.multiple_of(row, 16), rows), pl.ds(pl.multiple_of(column, 128), 640)],
+                    out_ref.at[pl.ds(pl.multiple_of(row, 32), CHUNK), pl.ds(pl.multiple_of(column, 128), 640)],
                     out_of.at[len(stores)],
                 )
                 store.start()
@@ -133,66 +135,39 @@
             + [pltpu.SemaphoreType.DMA((len(blocks),)), pltpu.SemaphoreType.DMA((count,))],
         ),
         input_output_aliases={} if into is None else {len(operands): 0},
-        name="lay",
+        compiler_params=pltpu.CompilerParams(vmem_limit_bytes=8 << 20),
     )(where, *operands)
 
 
 def first_moves(new_weight):
     rows = new_weight.shape[0] // 2
-    z, core = lax.axis_index("z"), lax.axis_index("k")
+    x, z, core = lax.axis_index("x"), lax.axis_index("z"), lax.axis_index("k")
     turned = new_weight.T
     other = lax.dynamic_slice(turned, (0, (1 - core) * rows), (turned.shape[0], rows))
-    chunks = turn(jnp.stack([core, z]).astype(jnp.int32), turned, swap_core(other))
+    chunks = turn(jnp.stack([core, x + z]).astype(jnp.int32), turned, swap_core(other))
     got = [to_owner(chunks[step], step) for step in range(4)]
-    own_a = jnp.stack([block[:ROWS_A] for block in got])
-    own_b = jnp.stack([block[ROWS_A:] for block in got])
-    return own_a, own_b
-
-
-def move_weight(own_a, own_b):
-    x, q = lax.axis_index("x"), lax.axis_index("q")
-    ya = swap_q(own_a)
-    a_m, a_p = along_x(own_a, 1), along_x(own_a, -1)
-    yb = swap_q(own_b)
-    b_m, b_p = along_x(own_b, 1), along_x(own_b, -1)
-    a_2 = along_x(a_m, 1)
-    b_2 = along_x(b_p, -1)
-    ya_m, ya_p = along_x(ya, 1), along_x(ya, -1)
-    ya_2 = along_x(ya_p, -1)
-    yb_m = swap_q(b_m)
-    yb_p = swap_q(b_p)
-    yb_2 = swap_q(b_2)
-    four = (0, 1, 2, 3)
-    where = jnp.stack([x, q]).astype(jnp.int32)
-    out = lay(
-        where,
-        [own_a, own_b, a_m, a_p, b_m, b_p, ya, yb],
-        [
-            (0, 0, four, 0),
-            (0, 0, four, ROWS_A),
-            (3, 0, four, 0),
-            (1, 0, four, 0),
-            (3, 0, four, ROWS_A),
-            (1, 0, four, ROWS_A),
-            (0, 1, four, 0),
-            (0, 1, four, ROWS_A),
-        ],
-    )
-    return lay(
-        where,
-        [a_2, b_2, ya_m, ya_p, yb_m, yb_p, ya_2, yb_2],
-        [
-            (2, 0, four, 0),
-            (2, 0, four, ROWS_A),
-            (3, 1, four, 0),
-            (1, 1, four, 0),
-            (3, 1, four, ROWS_A),
-            (1, 1, four, ROWS_A),
-            (2, 1, four, 0),
-            (2, 1, four, ROWS_A),
-        ],
-        out,
-    )
+    return jnp.stack(got[:2]), jnp.stack(got[2:])
+
+
+def move_weight(na, nb):
+    x, q, z = lax.axis_index("x"), lax.axis_index("q"), lax.axis_index("z")
+    fa, fb = swap_q(na), swap_q(nb)
+    na_m, na_p = along_x(na, 1), along_x(na, -1)
+    nb_m, nb_p = along_x(nb, 1), along_x(nb, -1)
+    na_2, nb_2 = along_x(na_m, 1), along_x(nb_p, -1)
+    fa_m, fa_p = along_x(fa, 1), along_x(fa, -1)
+    fb_m, fb_p = along_x(fb, 1), along_x(fb, -1)
+    fa_2, fb_2 = swap_q(na_2), swap_q(nb_2)
+    a, b = (0, 1), (2, 3)
+    where = jnp.stack([x, q, z]).astype(jnp.int32)
+    out = None
+    for spots in (
+        [(na, 0, 0, a), (nb, 0, 0, b), (na_m, 3, 0, a), (na_p, 1, 0, a), (na_2, 2, 0, a), (fa, 0, 1, a)],
+        [(nb_m, 3, 0, b), (nb_p, 1, 0, b), (fa_m, 3, 1, a), (fa_p, 1, 1, a), (fb, 0, 1, b)],
+        [(nb_2, 2, 0, b), (fa_2, 2, 1, a), (fb_m, 3, 1, b), (fb_p, 1, 1, b), (fb_2, 2, 1, b)],
+    ):
+        out = lay(where, [spot[0] for spot in spots], [spot[1:] for spot in spots], out)
+    return out
 
 
 def stats_kernel(ids_ref, near_ref, far_ref, weight_ref, out_ref, rows_ref, sems):
@@ -233,24 +208,52 @@
         out_ref[2:3] = out_ref[2:3] + found
 
 
-def part_stats(near, far, weight, ids):
-    count = 2 * near.shape[0]
-    tile = 384
+def row_stats(near, far, weight, ids):
+    half, width = near.shape
     anywhere = pl.BlockSpec(memory_space=pl.ANY)
     return pl.pallas_call(
         stats_kernel,
-        out_shape=jax.ShapeDtypeStruct((3, count), jnp.float32),
-        grid=(weight.shape[0] // tile,),
+        out_shape=jax.ShapeDtypeStruct((3, 2 * half), jnp.float32),
+        grid=(weight.shape[0] // TILE,),
         in_specs=[
-            pl.BlockSpec((1, count), lambda i: (0, 0)),
+            pl.BlockSpec((1, 2 * half), lambda i: (0, 0)),
             anywhere,
             anywhere,
-            pl.BlockSpec((tile, weight.shape[1]), lambda i: (i, 0)),
+            pl.BlockSpec((TILE, width), lambda i: (i, 0)),
         ],
-        out_specs=pl.BlockSpec((3, count), lambda i: (0, 0)),
-        scratch_shapes=[pltpu.VMEM((count, weight.shape[1]), near.dtype), pltpu.SemaphoreType.DMA((2,))],
+        out_specs=pl.BlockSpec((3, 2 * half), lambda i: (0, 0)),
+        scratch_shapes=[pltpu.VMEM((2 * half, width), near.dtype), pltpu.SemaphoreType.DMA((2,))],
+        compiler_params=pltpu.CompilerParams(vmem_limit_bytes=STATS_VMEM << 20),
         name="stats",
-    )(ids.reshape(1, count), near, far, weight)
+    )(ids.reshape(1, 2 * half), near, far, weight)
+
+
+def cat_kernel(*refs):
+    blocks, out_ref, stage, sems = refs[:-3], refs[-3], refs[-2], refs[-1]
+    rows = blocks[0].shape[0]
+    loads = [
+        pltpu.make_async_copy(block, stage.at[pl.ds(i * rows, rows)], sems.at[i]) for i, block in enumerate(blocks)
+    ]
+    for load in loads:
+        load.start()
+    for load in loads:
+        load.wait()
+    store = pltpu.make_async_copy(stage, out_ref, sems.at[len(blocks)])
+    store.start()
+    store.wait()
+
+
+def cat(blocks):
+    shape = (len(blocks) * blocks[0].shape[0], blocks[0].shape[1])
+    anywhere = pl.BlockSpec(memory_space=pl.ANY)
+    return pl.pallas_call(
+        cat_kernel,
+        out_shape=jax.ShapeDtypeStruct(shape, blocks[0].dtype),
+        in_specs=[anywhere] * len(blocks),
+        out_specs=anywhere,
+        scratch_shapes=[pltpu.VMEM(shape, blocks[0].dtype), pltpu.SemaphoreType.DMA((len(blocks) + 1,))],
+        compiler_params=pltpu.CompilerParams(vmem_limit_bytes=8 << 20),
+    )(*blocks)
 
 
 def by_owner(stats):
@@ -278,15 +281,13 @@
     m, p = along_z(hidden, 1), along_z(hidden, -1)
     flipped = swap_h(hidden)
     far = along_z(m, 1)
-    groups = [jnp.concatenate([hidden, m, far, p], axis=0)]
+    near = [hidden, m, far, p]
     m, p = along_z(flipped, 1), along_z(flipped, -1)
     far = along_z(p, -1)
-    groups.append(jnp.concatenate([flipped, m, far, p], axis=0))
-    stats = []
-    for flip, group in enumerate(groups):
-        ids = wanted[:, flip].transpose(1, 0, 2).reshape(-1)
-        stats.append(part_stats(group, swap_core(group), old_weight, ids).reshape(3, 2, 4, own_rows))
-    stats = jnp.stack(stats, axis=0).transpose(3, 0, 2, 1, 4)
+    near = cat(near + [flipped, m, far, p])
+    far = swap_core(near)
+    ids = wanted.transpose(2, 1, 0, 3)
+    stats = row_stats(near, far, old_weight, ids).reshape((3,) + ids.shape).transpose(3, 2, 1, 0, 4)
     stats = by_owner(stats).reshape(16, 3 * own_rows)
     stats = lax.all_to_all(stats, ("z", "h", "k"), split_axis=0, concat_axis=0, tiled=True)
     stats = stats.reshape(16, 3, own_rows)
@@ -297,8 +298,8 @@
 
 
 def on_device(hidden, tokens, old_weight, new_weight):
-    own_a, own_b = first_moves(new_weight)
-    return log_probs(hidden, tokens, old_weight), move_weight(own_a, own_b)
+    na, nb = first_moves(new_weight)
+    return log_probs(hidden, tokens, old_weight), move_weight(na, nb)
 
 
 def solution(mesh):

time: 235 us -> 248 us (1.055); the launches traced: 232 us -> 247 us
  waiting for transfers between devices: 87.1 us -> 124 us
  local copies, waits for them, and re-layouts: 18 us -> 6.7 us
  starting transfers between devices: 82.3 us -> 77.1 us
  Pallas kernels: 41.1 us -> 37.5 us
    ppermute x28 -> x27, waiting for transfers between devices: 86.4 us -> 124 us  [send(): return lax.ppermute(value, AXES, pairs(move))]
    unnamed x28 -> x14, local copies, waits for them, and re-layouts: 8.85 us -> 3.15 us
    ppermute x28 -> x27, starting transfers between devices: 71.7 us -> 66.8 us  [send(): return lax.ppermute(value, AXES, pairs(move))]
    concatenate x2 -> x0, local copies, waits for them, and re-layouts: 3.12 us -> none  [the longest x1 1.99 us: log_probs(): groups = [jnp.concatenate([hidden, m, far, p], axis=0)]]
    another operation x14 -> x0, local copies, waits for them, and re-layouts: 3.06 us -> none  [the longest x4 1.58 us: log_probs(): stats = jnp.stack(stats, axis=0).transpose(3, 0, 2, 1, 4)]
    pallas_call x1, Pallas kernels: 3.59 us -> 1.11 us  [turn(): pl.pallas_call(turn_kernel, out_shape=[jax.ShapeDtypeStruct((CHUNK, 2 * w...]
    pallas_call x2 -> x3, Pallas kernels: 11.8 us -> 11.6 us  [lay(): pl.pallas_call(laid(spots), out_shape=jax.ShapeDtypeStruct((4 * CHUNK, 51...]
  transfers between devices with their start and end apart: 29 -> 28, of which waited for: 10 -> 13; matrix products, arithmetic and copies ran while one was open for 7% -> 1% of each run, Pallas kernels for 18% -> 14%
where the time goes in v2:
time: 248 us; the launch traced here: 247 us
  waiting for transfers between devices  124 us (50%)
  starting transfers between devices  77.1 us (31%)
  Pallas kernels  37.5 us (15%)
  local copies, waits for them, and re-layouts  6.7 us (3%)
    ppermute x27, waiting for transfers between devices, send(): return lax.ppermute(value, AXES, pairs(move))  124 us
    ppermute x27, starting transfers between devices, send(): return lax.ppermute(value, AXES, pairs(move))  66.8 us
    pallas_call x1, Pallas kernels, row_stats(): pl.pallas_call(stats_kernel, out_shape=jax.ShapeDtypeStruct((3, 2 * half)...  20.8 us
    pallas_call x3, Pallas kernels, lay(): pl.pallas_call(laid(spots), out_shape=jax.ShapeDtypeStruct((4 * CHUNK, 51...  11.6 us
    all_to_all x1, starting transfers between devices, log_probs(): lax.all_to_all(stats, ('z', 'h', 'k'), split_axis=0, concat_axis=0, tiled...  10.3 us
  transfers between devices with their start and end apart: 28, of which 13 were waited for; matrix products, arithmetic and copies ran while one was open for 1% of the time, Pallas kernels for 14%

profile of v2, /device:TPU:1, one launch (start us, length us, event | category | flops | bytes accessed | tf_op | source)
XLA Modules:
  0.0 247.2 jit_solution(945109613696959923)
XLA Ops:
  0.6 3.8 %collective-permute-start.3 = (bf16[64,5120]{1,0:T(8,128)(2,1)}, bf16[64,5120]{1,0:T(8,128)(2,1)S(1)}, u32[]{:S(2)}, u32[]{:S(2)}) collective-permute-start(bf16[64,5120]{1,0:T(8,128)(2,1)} %refs_0_.1), channel_id=1, source_target_pairs={{0,2},{1,3},{2,0},{3,1},{4,6},{5,7},{6,4},{7,5},{8,10},{9,11},{10,... | collective-permute-start | bytes 1966088 | tf_op jit(solution)/shard_map/ppermute | solution.py:33
  6.1 12.8 %collective-permute-done.3.refs_4_ = bf16[64,5120]{1,0:T(8,128)(2,1)S(1)} collective-permute-done((bf16[64,5120]{1,0:T(8,128)(2,1)}, bf16[64,5120]{1,0:T(8,128)(2,1)S(1)}, u32[]{:S(2)}, u32[]{:S(2)}) %collective-permute-start.3) | collective-permute-done | bytes 655392 | tf_op jit(solution)/shard_map/ppermute | solution.py:33
  18.9 3.7 %collective-permute-start.5 = (bf16[64,5120]{1,0:T(8,128)(2,1)S(1)}, bf16[64,5120]{1,0:T(8,128)(2,1)S(1)}, u32[]{:S(2)}, u32[]{:S(2)}) collective-permute-start(bf16[64,5120]{1,0:T(8,128)(2,1)S(1)} %collective-permute-done.3.refs_4_), channel_id=1, source_target_pairs={{0,12},{1,13},{2,14},{3,15},{4,0},{5,1},{6,2},{7,3},{8,4},{9,5},{1... | collective-permute-start | bytes 1966088 | tf_op jit(solution)/shard_map/ppermute | solution.py:33
  24.1 11.1 %collective-permute-done.5.refs_7_ = bf16[64,5120]{1,0:T(8,128)(2,1)S(1)} collective-permute-done((bf16[64,5120]{1,0:T(8,128)(2,1)S(1)}, bf16[64,5120]{1,0:T(8,128)(2,1)S(1)}, u32[]{:S(2)}, u32[]{:S(2)}) %collective-permute-start.5) | collective-permute-done | bytes 655392 | tf_op jit(solution)/shard_map/ppermute | solution.py:33
  38.6 10.7 %collective-permute-done.2.refs_3_ = bf16[64,5120]{1,0:T(8,128)(2,1)S(1)} collective-permute-done((bf16[64,5120]{1,0:T(8,128)(2,1)}, bf16[64,5120]{1,0:T(8,128)(2,1)S(1)}, u32[]{:S(2)}, u32[]{:S(2)}) %collective-permute-start.2) | collective-permute-done | bytes 655392 | tf_op jit(solution)/shard_map/ppermute | solution.py:33
  52.2 11.1 %collective-permute-done.6.refs_6_ = bf16[64,5120]{1,0:T(8,128)(2,1)S(1)} collective-permute-done((bf16[64,5120]{1,0:T(8,128)(2,1)S(1)}, bf16[64,5120]{1,0:T(8,128)(2,1)S(1)}, u32[]{:S(2)}, u32[]{:S(2)}) %collective-permute-start.6) | collective-permute-done | bytes 655392 | tf_op jit(solution)/shard_map/ppermute | solution.py:33
  64.4 4.1 %shard_map.59.near_ref = bf16[512,5120]{1,0:T(8,128)(2,1)} custom-call(bf16[64,5120]{1,0:T(8,128)(2,1)S(1)} %copy-done.5, bf16[64,5120]{1,0:T(8,128)(2,1)S(1)} %collective-permute-done.refs_1_, bf16[64,5120]{1,0:T(8,128)(2,1)S(1)} %collective-permute-done.1.refs_2_, bf16[64,5120]{1,0:T(8,128)(2,1)S(1)} %collective-permute-done.2.refs_3_, ...), custom_call_target="tpu_custom_call" | custom-call | tf_op jit(solution)/shard_map/pallas_call | solution.py:249
  72.3 8.2 %collective-permute-done.8.got_ref = bf16[320,1152]{1,0:T(8,128)(2,1)S(1)} collective-permute-done((bf16[320,1152]{1,0:T(8,128)(2,1)S(1)}, bf16[320,1152]{1,0:T(8,128)(2,1)S(1)}, u32[]{:S(2)}, u32[]{:S(2)}) %collective-permute-start.8) | collective-permute-done | bytes 737312 | tf_op jit(solution)/shard_map/ppermute | solution.py:33
  82.3 4.6 %collective-permute-start.14 = (bf16[288,640]{1,0:T(8,128)(2,1)S(1)}, bf16[288,640]{1,0:T(8,128)(2,1)S(1)}, u32[]{:S(2)}, u32[]{:S(2)}) collective-permute-start(bf16[288,640]{1,0:T(8,128)(2,1)S(1)} %get-tuple-element.9), channel_id=1, source_target_pairs={{0,32},{1,33},{2,48},{3,49},{4,64},{5,65},{6,80},{7,81},{8,96},{9,... | collective-permute-start | bytes 1105928 | tf_op jit(solution)/shard_map/ppermute | solution.py:33
  86.9 11.7 %collective-permute-done.14 = bf16[288,640]{1,0:T(8,128)(2,1)S(1)} collective-permute-done((bf16[288,640]{1,0:T(8,128)(2,1)S(1)}, bf16[288,640]{1,0:T(8,128)(2,1)S(1)}, u32[]{:S(2)}, u32[]{:S(2)}) %collective-permute-start.14) | collective-permute-done | bytes 368672 | tf_op jit(solution)/shard_map/ppermute | solution.py:33
  98.8 12.0 %collective-permute-start.9 = (bf16[288,640]{1,0:T(8,128)(2,1)S(1)}, bf16[288,640]{1,0:T(8,128)(2,1)S(1)}, u32[]{:S(2)}, u32[]{:S(2)}) collective-permute-start(bf16[288,640]{1,0:T(8,128)(2,1)S(1)} %get-tuple-element.6), channel_id=1, source_target_pairs={{0,64},{1,65},{2,80},{3,81},{4,96},{5,97},{6,112},{7,113},{8,0},{9... | collective-permute-start | bytes 1105928 | tf_op jit(solution)/shard_map/ppermute | solution.py:33
  110.8 3.8 %collective-permute-start.10 = (bf16[288,640]{1,0:T(8,128)(2,1)S(1)}, bf16[288,640]{1,0:T(8,128)(2,1)S(1)}, u32[]{:S(2)}, u32[]{:S(2)}) collective-permute-start(bf16[288,640]{1,0:T(8,128)(2,1)S(1)} %get-tuple-element.7), channel_id=1, source_target_pairs={{0,96},{1,97},{2,112},{3,113},{4,0},{5,1},{6,16},{7,17},{8,32},{9,... | collective-permute-start | bytes 1105928 | tf_op jit(solution)/shard_map/ppermute | solution.py:33
  117.8 3.8 %collective-permute-done.9 = bf16[288,640]{1,0:T(8,128)(2,1)S(1)} collective-permute-done((bf16[288,640]{1,0:T(8,128)(2,1)S(1)}, bf16[288,640]{1,0:T(8,128)(2,1)S(1)}, u32[]{:S(2)}, u32[]{:S(2)}) %collective-permute-start.9) | collective-permute-done | bytes 368672 | tf_op jit(solution)/shard_map/ppermute | solution.py:33
  124.9 9.8 %collective-permute-start.18 = (bf16[2,288,640]{2,1,0:T(8,128)(2,1)S(1)}, bf16[2,288,640]{2,1,0:T(8,128)(2,1)S(1)}, u32[]{:S(2)}, u32[]{:S(2)}) collective-permute-start(bf16[2,288,640]{2,1,0:T(8,128)(2,1)S(1)} %pad_maximum_fusion.refs_1_), channel_id=1, source_target_pairs={{0,16},{1,17},{2,18},{3,19},{4,20},{5,21},{6,22},{7,23},{8,24},{9,... | collective-permute-start | bytes 2211848 | tf_op jit(solution)/shard_map/ppermute | solution.py:33
  134.7 5.5 %collective-permute-start.11 = (bf16[2,288,640]{2,1,0:T(8,128)(2,1)S(1)}, bf16[2,288,640]{2,1,0:T(8,128)(2,1)}, u32[]{:S(2)}, u32[]{:S(2)}) collective-permute-start(bf16[2,288,640]{2,1,0:T(8,128)(2,1)S(1)} %pad_maximum_fusion.refs_1_), channel_id=1, source_target_pairs={{0,96},{1,97},{2,98},{3,99},{4,100},{5,101},{6,102},{7,103},{8,104... | collective-permute-start | bytes 2211848 | tf_op jit(solution)/shard_map/ppermute | solution.py:33
  143.2 10.0 %collective-permute-done.26.refs_3_ = bf16[2,288,640]{2,1,0:T(8,128)(2,1)S(1)} collective-permute-done((bf16[2,288,640]{2,1,0:T(8,128)(2,1)S(1)}, bf16[2,288,640]{2,1,0:T(8,128)(2,1)S(1)}, u32[]{:S(2)}, u32[]{:S(2)}) %collective-permute-start.26) | collective-permute-done | bytes 737312 | tf_op jit(solution)/shard_map/ppermute | solution.py:33
  157.9 11.2 %collective-permute-done.11.refs_1_ = bf16[2,288,640]{2,1,0:T(8,128)(2,1)} collective-permute-done((bf16[2,288,640]{2,1,0:T(8,128)(2,1)S(1)}, bf16[2,288,640]{2,1,0:T(8,128)(2,1)}, u32[]{:S(2)}, u32[]{:S(2)}) %collective-permute-start.11) | collective-permute-done | bytes 737312 | tf_op jit(solution)/shard_map/ppermute | solution.py:33
  170.3 11.4 %collective-permute-done.16.refs_4_ = bf16[2,288,640]{2,1,0:T(8,128)(2,1)} collective-permute-done((bf16[2,288,640]{2,1,0:T(8,128)(2,1)S(1)}, bf16[2,288,640]{2,1,0:T(8,128)(2,1)}, u32[]{:S(2)}, u32[]{:S(2)}) %collective-permute-start.16) | collective-permute-done | bytes 737312 | tf_op jit(solution)/shard_map/ppermute | solution.py:33
  181.7 15.8 %collective-permute-done.24.refs_2_ = bf16[2,288,640]{2,1,0:T(8,128)(2,1)} collective-permute-done((bf16[2,288,640]{2,1,0:T(8,128)(2,1)S(1)}, bf16[2,288,640]{2,1,0:T(8,128)(2,1)}, u32[]{:S(2)}, u32[]{:S(2)}) %collective-permute-start.24) | collective-permute-done | bytes 737312 | tf_op jit(solution)/shard_map/ppermute | solution.py:33
  200.8 20.8 %stats.1 = f32[3,1024]{1,0:T(4,128)} custom-call(s32[1,1024]{1,0:T(1,128)} %reshape.23.ids_ref, bf16[512,5120]{1,0:T(8,128)(2,1)} %shard_map.59.near_ref, bf16[512,5120]{1,0:T(8,128)(2,1)} %collective-permute-done.7.far_ref, bf16[1152,5120]{1,0:T(8,128)(2,1)} %weight_ref.1), custom_call_target="tpu_custom_call" | custom-call | tf_op jit(solution)/shard_map/stats/pallas_call | solution.py:214
  223.2 10.3 %all-to-all-start = ((f32[16,1,192]{2,1,0:T(1,128)}), f32[16,1,192]{2,1,0:T(1,128)S(1)}, u32[]{:S(2)}, u32[]{:S(2)}) async-start(f32[16,1,192]{2,1,0:T(1,128)} %all_to_all.8), calls=%async_computation | async-start | bytes 32768 | tf_op jit(solution)/shard_map/all_to_all | solution.py:292
  234.7 4.3 %shard_map.60.refs_5_ = bf16[1152,5120]{1,0:T(8,128)(2,1)} custom-call(s32[3]{0:T(128)S(1)} %pad_add_fusion.where_ref, bf16[2,288,640]{2,1,0:T(8,128)(2,1)S(1)} %pad_maximum_fusion.1.refs_0_, bf16[2,288,640]{2,1,0:T(8,128)(2,1)S(1)} %pad_maximum_fusion.refs_1_, bf16[2,288,640]{2,1,0:T(8,128)(2,1)S(1)} %collective-permute-done.15.refs_2_, ...), custom_call_target="tpu_custom_call" | custom-call | tf_op jit(solution)/shard_map/pallas_call | solution.py:126
  239.1 3.6 %shard_map.61.refs_5_ = bf16[1152,5120]{1,0:T(8,128)(2,1)} custom-call(s32[3]{0:T(128)S(1)} %pad_add_fusion.where_ref, bf16[2,288,640]{2,1,0:T(8,128)(2,1)} %collective-permute-done.22.refs_0_, bf16[2,288,640]{2,1,0:T(8,128)(2,1)} %collective-permute-done.11.refs_1_, ...), custom_call_target="tpu_custom_call", output_to_operand_aliasing={{}: (6, {})} | custom-call | tf_op jit(solution)/shard_map/pallas_call | solution.py:126
  242.8 3.6 %shard_map.62 = bf16[1152,5120]{1,0:T(8,128)(2,1)} custom-call(s32[3]{0:T(128)S(1)} %pad_add_fusion.where_ref, bf16[2,288,640]{2,1,0:T(8,128)(2,1)} %collective-permute-done.12.refs_0_, bf16[2,288,640]{2,1,0:T(8,128)(2,1)} %collective-permute-done.17.refs_1_, bf16[2,288,640]{2,1,0:T(8,128)(2,1)} %collective-permute-done.19.refs_2_, ...), custom_call_target="tpu_custom_call", output_to_operand_aliasing={{}: (6, {})} | custom-call | tf_op jit(solution)/shard_map/pallas_call | solution.py:126
  (78 shorter events, 38.4 us)
Async XLA Ops:
  0.6 18.2 %collective-permute-start.3 = (bf16[64,5120]{1,0:T(8,128)(2,1)}, bf16[64,5120]{1,0:T(8,128)(2,1)S(1)}, u32[]{:S(2)}, u32[]{:S(2)}) collective-permute-start(bf16[64,5120]{1,0:T(8,128)(2,1)} %refs_0_.1), channel_id=1, source_target_pairs={{0,2},{1,3},{2,0},{3,1},{4,6},{5,7},{6,4},{7,5},{8,10},{9,11},{10,... | collective-permute-start | bytes 1966088 | tf_op jit(solution)/shard_map/ppermute | solution.py:33
  4.5 19.6 %collective-permute-start = (bf16[64,5120]{1,0:T(8,128)(2,1)}, bf16[64,5120]{1,0:T(8,128)(2,1)S(1)}, u32[]{:S(2)}, u32[]{:S(2)}) collective-permute-start(bf16[64,5120]{1,0:T(8,128)(2,1)} %refs_0_.1), channel_id=1, source_target_pairs={{0,4},{1,5},{2,6},{3,7},{4,8},{5,9},{6,10},{7,11},{8,12},{9,13},{1... | collective-permute-start | bytes 1966088 | tf_op jit(solution)/shard_map/ppermute | solution.py:33
  22.6 26.7 %collective-permute-start.2 = (bf16[64,5120]{1,0:T(8,128)(2,1)}, bf16[64,5120]{1,0:T(8,128)(2,1)S(1)}, u32[]{:S(2)}, u32[]{:S(2)}) collective-permute-start(bf16[64,5120]{1,0:T(8,128)(2,1)} %refs_0_.1), channel_id=1, source_target_pairs={{0,12},{1,13},{2,14},{3,15},{4,0},{5,1},{6,2},{7,3},{8,4},{9,5},{1... | collective-permute-start | bytes 1966088 | tf_op jit(solution)/shard_map/ppermute | solution.py:33
  22.8 26.6 %collective-permute-start.4 = (bf16[64,5120]{1,0:T(8,128)(2,1)S(1)}, bf16[64,5120]{1,0:T(8,128)(2,1)S(1)}, u32[]{:S(2)}, u32[]{:S(2)}) collective-permute-start(bf16[64,5120]{1,0:T(8,128)(2,1)S(1)} %collective-permute-done.3.refs_4_), channel_id=1, source_target_pairs={{0,4},{1,5},{2,6},{3,7},{4,8},{5,9},{6,10},{7,11},{8,12},{9,13},{1... | collective-permute-start | bytes 1966088 | tf_op jit(solution)/shard_map/ppermute | solution.py:33
  24.1 28.1 %collective-permute-start.1 = (bf16[64,5120]{1,0:T(8,128)(2,1)S(1)}, bf16[64,5120]{1,0:T(8,128)(2,1)S(1)}, u32[]{:S(2)}, u32[]{:S(2)}) collective-permute-start(bf16[64,5120]{1,0:T(8,128)(2,1)S(1)} %collective-permute-done.refs_1_), channel_id=1, source_target_pairs={{0,4},{1,5},{2,6},{3,7},{4,8},{5,9},{6,10},{7,11},{8,12},{9,13},{1... | collective-permute-start | bytes 1966088 | tf_op jit(solution)/shard_map/ppermute | solution.py:33
  35.2 28.1 %collective-permute-start.6 = (bf16[64,5120]{1,0:T(8,128)(2,1)S(1)}, bf16[64,5120]{1,0:T(8,128)(2,1)S(1)}, u32[]{:S(2)}, u32[]{:S(2)}) collective-permute-start(bf16[64,5120]{1,0:T(8,128)(2,1)S(1)} %collective-permute-done.5.refs_7_), channel_id=1, source_target_pairs={{0,12},{1,13},{2,14},{3,15},{4,0},{5,1},{6,2},{7,3},{8,4},{9,5},{1... | collective-permute-start | bytes 1966088 | tf_op jit(solution)/shard_map/ppermute | solution.py:33
  68.5 130.6 %collective-permute-start.7 = (bf16[512,5120]{1,0:T(8,128)(2,1)}, bf16[512,5120]{1,0:T(8,128)(2,1)}, u32[]{:S(2)}, u32[]{:S(2)}) collective-permute-start(bf16[512,5120]{1,0:T(8,128)(2,1)} %shard_map.59.near_ref), channel_id=1, source_target_pairs={{0,1},{1,0},{2,3},{3,2},{4,5},{5,4},{6,7},{7,6},{8,9},{9,8},{10,11... | collective-permute-start | bytes 15728648 | tf_op jit(solution)/shard_map/ppermute | solution.py:33
  82.3 16.3 %collective-permute-start.14 = (bf16[288,640]{1,0:T(8,128)(2,1)S(1)}, bf16[288,640]{1,0:T(8,128)(2,1)S(1)}, u32[]{:S(2)}, u32[]{:S(2)}) collective-permute-start(bf16[288,640]{1,0:T(8,128)(2,1)S(1)} %get-tuple-element.9), channel_id=1, source_target_pairs={{0,32},{1,33},{2,48},{3,49},{4,64},{5,65},{6,80},{7,81},{8,96},{9,... | collective-permute-start | bytes 1105928 | tf_op jit(solution)/shard_map/ppermute | solution.py:33
  98.7 36.0 %collective-permute-start.15 = (bf16[2,288,640]{2,1,0:T(8,128)(2,1)S(1)}, bf16[2,288,640]{2,1,0:T(8,128)(2,1)S(1)}, u32[]{:S(2)}, u32[]{:S(2)}) collective-permute-start(bf16[2,288,640]{2,1,0:T(8,128)(2,1)S(1)} %pad_maximum_fusion.1.refs_0_), channel_id=1, source_target_pairs={{0,32},{1,33},{2,34},{3,35},{4,36},{5,37},{6,38},{7,39},{8,40},{9,... | collective-permute-start | bytes 2211848 | tf_op jit(solution)/shard_map/ppermute | solution.py:33
  98.8 22.8 %collective-permute-start.9 = (bf16[288,640]{1,0:T(8,128)(2,1)S(1)}, bf16[288,640]{1,0:T(8,128)(2,1)S(1)}, u32[]{:S(2)}, u32[]{:S(2)}) collective-permute-start(bf16[288,640]{1,0:T(8,128)(2,1)S(1)} %get-tuple-element.6), channel_id=1, source_target_pairs={{0,64},{1,65},{2,80},{3,81},{4,96},{5,97},{6,112},{7,113},{8,0},{9... | collective-permute-start | bytes 1105928 | tf_op jit(solution)/shard_map/ppermute | solution.py:33
  114.6 25.6 %collective-permute-start.23 = (bf16[2,288,640]{2,1,0:T(8,128)(2,1)S(1)}, bf16[2,288,640]{2,1,0:T(8,128)(2,1)S(1)}, u32[]{:S(2)}, u32[]{:S(2)}) collective-permute-start(bf16[2,288,640]{2,1,0:T(8,128)(2,1)S(1)} %pad_maximum_fusion.1.refs_0_), channel_id=1, source_target_pairs={{0,16},{1,17},{2,18},{3,19},{4,20},{5,21},{6,22},{7,23},{8,24},{9,... | collective-permute-start | bytes 2211848 | tf_op jit(solution)/shard_map/ppermute | solution.py:33
  121.6 31.6 %collective-permute-start.26 = (bf16[2,288,640]{2,1,0:T(8,128)(2,1)S(1)}, bf16[2,288,640]{2,1,0:T(8,128)(2,1)S(1)}, u32[]{:S(2)}, u32[]{:S(2)}) collective-permute-start(bf16[2,288,640]{2,1,0:T(8,128)(2,1)S(1)} %pad_maximum_fusion.1.refs_0_), channel_id=1, source_target_pairs={{0,96},{1,97},{2,98},{3,99},{4,100},{5,101},{6,102},{7,103},{8,104... | collective-permute-start | bytes 2211848 | tf_op jit(solution)/shard_map/ppermute | solution.py:33
  124.9 30.5 %collective-permute-start.18 = (bf16[2,288,640]{2,1,0:T(8,128)(2,1)S(1)}, bf16[2,288,640]{2,1,0:T(8,128)(2,1)S(1)}, u32[]{:S(2)}, u32[]{:S(2)}) collective-permute-start(bf16[2,288,640]{2,1,0:T(8,128)(2,1)S(1)} %pad_maximum_fusion.refs_1_), channel_id=1, source_target_pairs={{0,16},{1,17},{2,18},{3,19},{4,20},{5,21},{6,22},{7,23},{8,24},{9,... | collective-permute-start | bytes 2211848 | tf_op jit(solution)/shard_map/ppermute | solution.py:33
  134.7 34.4 %collective-permute-start.11 = (bf16[2,288,640]{2,1,0:T(8,128)(2,1)S(1)}, bf16[2,288,640]{2,1,0:T(8,128)(2,1)}, u32[]{:S(2)}, u32[]{:S(2)}) collective-permute-start(bf16[2,288,640]{2,1,0:T(8,128)(2,1)S(1)} %pad_maximum_fusion.refs_1_), channel_id=1, source_target_pairs={{0,96},{1,97},{2,98},{3,99},{4,100},{5,101},{6,102},{7,103},{8,104... | collective-permute-start | bytes 2211848 | tf_op jit(solution)/shard_map/ppermute | solution.py:33
  140.2 29.0 %collective-permute-start.22 = (bf16[2,288,640]{2,1,0:T(8,128)(2,1)S(1)}, bf16[2,288,640]{2,1,0:T(8,128)(2,1)}, u32[]{:S(2)}, u32[]{:S(2)}) collective-permute-start(bf16[2,288,640]{2,1,0:T(8,128)(2,1)S(1)} %pad_maximum_fusion.refs_1_), channel_id=1, source_target_pairs={{0,32},{1,33},{2,34},{3,35},{4,36},{5,37},{6,38},{7,39},{8,40},{9,... | collective-permute-start | bytes 2211848 | tf_op jit(solution)/shard_map/ppermute | solution.py:33
  154.1 27.5 %collective-permute-start.16 = (bf16[2,288,640]{2,1,0:T(8,128)(2,1)S(1)}, bf16[2,288,640]{2,1,0:T(8,128)(2,1)}, u32[]{:S(2)}, u32[]{:S(2)}) collective-permute-start(bf16[2,288,640]{2,1,0:T(8,128)(2,1)S(1)} %collective-permute-done.15.refs_2_), channel_id=1, source_target_pairs={{0,32},{1,33},{2,34},{3,35},{4,36},{5,37},{6,38},{7,39},{8,40},{9,... | collective-permute-start | bytes 2211848 | tf_op jit(solution)/shard_map/ppermute | solution.py:33
  155.4 42.1 %collective-permute-start.24 = (bf16[2,288,640]{2,1,0:T(8,128)(2,1)S(1)}, bf16[2,288,640]{2,1,0:T(8,128)(2,1)}, u32[]{:S(2)}, u32[]{:S(2)}) collective-permute-start(bf16[2,288,640]{2,1,0:T(8,128)(2,1)S(1)} %collective-permute-done.23.refs_5_), channel_id=1, source_target_pairs={{0,32},{1,33},{2,34},{3,35},{4,36},{5,37},{6,38},{7,39},{8,40},{9,... | collective-permute-start | bytes 2211848 | tf_op jit(solution)/shard_map/ppermute | solution.py:33
  169.1 29.6 %collective-permute-start.12 = (bf16[2,288,640]{2,1,0:T(8,128)(2,1)}, bf16[2,288,640]{2,1,0:T(8,128)(2,1)}, u32[]{:S(2)}, u32[]{:S(2)}) collective-permute-start(bf16[2,288,640]{2,1,0:T(8,128)(2,1)} %collective-permute-done.11.refs_1_), channel_id=1, source_target_pairs={{0,96},{1,97},{2,98},{3,99},{4,100},{5,101},{6,102},{7,103},{8,104... | collective-permute-start | bytes 2211848 | tf_op jit(solution)/shard_map/ppermute | solution.py:33
  169.3 69.8 %collective-permute-start.25 = (bf16[2,288,640]{2,1,0:T(8,128)(2,1)S(1)}, bf16[2,288,640]{2,1,0:T(8,128)(2,1)}, u32[]{:S(2)}, u32[]{:S(2)}) collective-permute-start(bf16[2,288,640]{2,1,0:T(8,128)(2,1)S(1)} %collective-permute-done.23.refs_5_), channel_id=1, source_target_pairs={{0,96},{1,97},{2,98},{3,99},{4,100},{5,101},{6,102},{7,103},{8,104... | collective-permute-start | bytes 2211848 | tf_op jit(solution)/shard_map/ppermute | solution.py:33
  181.7 61.1 %collective-permute-start.19 = (bf16[2,288,640]{2,1,0:T(8,128)(2,1)}, bf16[2,288,640]{2,1,0:T(8,128)(2,1)}, u32[]{:S(2)}, u32[]{:S(2)}) collective-permute-start(bf16[2,288,640]{2,1,0:T(8,128)(2,1)} %copy-done.3), channel_id=1, source_target_pairs={{0,32},{1,33},{2,34},{3,35},{4,36},{5,37},{6,38},{7,39},{8,40},{9,... | collective-permute-start | bytes 2211848 | tf_op jit(solution)/shard_map/ppermute | solution.py:33
  197.5 45.3 %collective-permute-start.20 = (bf16[2,288,640]{2,1,0:T(8,128)(2,1)}, bf16[2,288,640]{2,1,0:T(8,128)(2,1)}, u32[]{:S(2)}, u32[]{:S(2)}) collective-permute-start(bf16[2,288,640]{2,1,0:T(8,128)(2,1)} %copy-done.3), channel_id=1, source_target_pairs={{0,96},{1,97},{2,98},{3,99},{4,100},{5,101},{6,102},{7,103},{8,104... | collective-permute-start | bytes 2211848 | tf_op jit(solution)/shard_map/ppermute | solution.py:33
  198.6 44.1 %collective-permute-start.17 = (bf16[2,288,640]{2,1,0:T(8,128)(2,1)}, bf16[2,288,640]{2,1,0:T(8,128)(2,1)}, u32[]{:S(2)}, u32[]{:S(2)}) collective-permute-start(bf16[2,288,640]{2,1,0:T(8,128)(2,1)} %collective-permute-done.16.refs_4_), channel_id=1, source_target_pairs={{0,16},{1,17},{2,18},{3,19},{4,20},{5,21},{6,22},{7,23},{8,24},{9,... | collective-permute-start | bytes 2211848 | tf_op jit(solution)/shard_map/ppermute | solution.py:33
  199.0 43.8 %collective-permute-start.21 = (bf16[2,288,640]{2,1,0:T(8,128)(2,1)}, bf16[2,288,640]{2,1,0:T(8,128)(2,1)}, u32[]{:S(2)}, u32[]{:S(2)}) collective-permute-start(bf16[2,288,640]{2,1,0:T(8,128)(2,1)} %collective-permute-done.12.refs_0_), channel_id=1, source_target_pairs={{0,16},{1,17},{2,18},{3,19},{4,20},{5,21},{6,22},{7,23},{8,24},{9,... | collective-permute-start | bytes 2211848 | tf_op jit(solution)/shard_map/ppermute | solution.py:33
  223.2 23.2 %all-to-all-start = ((f32[16,1,192]{2,1,0:T(1,128)}), f32[16,1,192]{2,1,0:T(1,128)S(1)}, u32[]{:S(2)}, u32[]{:S(2)}) async-start(f32[16,1,192]{2,1,0:T(1,128)} %all_to_all.8), calls=%async_computation | async-start | bytes 32768 | tf_op jit(solution)/shard_map/all_to_all | solution.py:292
  (11 other events, 249.7 us)

commit v3 on v2

--- a/solution.py
+++ b/solution.py
@@ -146,44 +146,36 @@
     other = lax.dynamic_slice(turned, (0, (1 - core) * rows), (turned.shape[0], rows))
     chunks = turn(jnp.stack([core, x + z]).astype(jnp.int32), turned, swap_core(other))
     got = [to_owner(chunks[step], step) for step in range(4)]
-    return jnp.stack(got[:2]), jnp.stack(got[2:])
-
-
-def move_weight(na, nb):
+    return jnp.stack(got)
+
+
+def move_weight(n):
     x, q, z = lax.axis_index("x"), lax.axis_index("q"), lax.axis_index("z")
-    fa, fb = swap_q(na), swap_q(nb)
-    na_m, na_p = along_x(na, 1), along_x(na, -1)
-    nb_m, nb_p = along_x(nb, 1), along_x(nb, -1)
-    na_2, nb_2 = along_x(na_m, 1), along_x(nb_p, -1)
-    fa_m, fa_p = along_x(fa, 1), along_x(fa, -1)
-    fb_m, fb_p = along_x(fb, 1), along_x(fb, -1)
+    f = swap_q(n)
+    n_m, n_p = along_x(n, 1), along_x(n, -1)
+    na_2, nb_2 = along_x(n_m[:2], 1), along_x(n_p[2:], -1)
+    f_m, f_p = along_x(f, 1), along_x(f, -1)
     fa_2, fb_2 = swap_q(na_2), swap_q(nb_2)
-    a, b = (0, 1), (2, 3)
+    a, b, ab = (0, 1), (2, 3), (0, 1, 2, 3)
     where = jnp.stack([x, q, z]).astype(jnp.int32)
     out = None
     for spots in (
-        [(na, 0, 0, a), (nb, 0, 0, b), (na_m, 3, 0, a), (na_p, 1, 0, a), (na_2, 2, 0, a), (fa, 0, 1, a)],
-        [(nb_m, 3, 0, b), (nb_p, 1, 0, b), (fa_m, 3, 1, a), (fa_p, 1, 1, a), (fb, 0, 1, b)],
-        [(nb_2, 2, 0, b), (fa_2, 2, 1, a), (fb_m, 3, 1, b), (fb_p, 1, 1, b), (fb_2, 2, 1, b)],
+        [(n, 0, 0, ab), (n_m, 3, 0, ab), (n_p, 1, 0, ab), (f, 0, 1, ab)],
+        [(na_2, 2, 0, a), (nb_2, 2, 0, b), (fa_2, 2, 1, a), (fb_2, 2, 1, b)],
+        [(f_m, 3, 1, ab), (f_p, 1, 1, ab)],
     ):
         out = lay(where, [spot[0] for spot in spots], [spot[1:] for spot in spots], out)
     return out
 
 
-def stats_kernel(ids_ref, near_ref, far_ref, weight_ref, out_ref, rows_ref, sems):
+def stats_kernel(ids_ref, hidden_ref, weight_ref, out_ref, rows_ref, sem):
     step = pl.program_id(0)
-    half = near_ref.shape[0]
 
     @pl.when(step == 0)
     def _():
-        copies = [
-            pltpu.make_async_copy(near_ref, rows_ref.at[pl.ds(0, half)], sems.at[0]),
-            pltpu.make_async_copy(far_ref, rows_ref.at[pl.ds(half, half)], sems.at[1]),
-        ]
-        for copy in copies:
-            copy.start()
-        for copy in copies:
-            copy.wait()
+        copy = pltpu.make_async_copy(hidden_ref, rows_ref, sem)
+        copy.start()
+        copy.wait()
 
     logits = lax.dot_general(
         weight_ref[...], rows_ref[...], (((1,), (1,)), ((), ())), preferred_element_type=jnp.float32
@@ -208,24 +200,21 @@
         out_ref[2:3] = out_ref[2:3] + found
 
 
-def row_stats(near, far, weight, ids):
-    half, width = near.shape
-    anywhere = pl.BlockSpec(memory_space=pl.ANY)
+def row_stats(rows, weight, ids):
+    count, width = rows.shape
     return pl.pallas_call(
         stats_kernel,
-        out_shape=jax.ShapeDtypeStruct((3, 2 * half), jnp.float32),
+        out_shape=jax.ShapeDtypeStruct((3, count), jnp.float32),
         grid=(weight.shape[0] // TILE,),
         in_specs=[
-            pl.BlockSpec((1, 2 * half), lambda i: (0, 0)),
-            anywhere,
-            anywhere,
+            pl.BlockSpec((1, count), lambda i: (0, 0)),
+            pl.BlockSpec(memory_space=pl.ANY),
             pl.BlockSpec((TILE, width), lambda i: (i, 0)),
         ],
-        out_specs=pl.BlockSpec((3, 2 * half), lambda i: (0, 0)),
-        scratch_shapes=[pltpu.VMEM((2 * half, width), near.dtype), pltpu.SemaphoreType.DMA((2,))],
+        out_specs=pl.BlockSpec((3, count), lambda i: (0, 0)),
+        scratch_shapes=[pltpu.VMEM((count, width), rows.dtype), pltpu.SemaphoreType.DMA(())],
         compiler_params=pltpu.CompilerParams(vmem_limit_bytes=STATS_VMEM << 20),
-        name="stats",
-    )(ids.reshape(1, 2 * half), near, far, weight)
+    )(ids.reshape(1, count), rows, weight)
 
 
 def cat_kernel(*refs):
@@ -287,7 +276,8 @@
     near = cat(near + [flipped, m, far, p])
     far = swap_core(near)
     ids = wanted.transpose(2, 1, 0, 3)
-    stats = row_stats(near, far, old_weight, ids).reshape((3,) + ids.shape).transpose(3, 2, 1, 0, 4)
+    stats = [row_stats(rows, old_weight, ids[flip]) for flip, rows in enumerate((near, far))]
+    stats = jnp.stack(stats).reshape(2, 3, 2, 4, own_rows).transpose(3, 2, 0, 1, 4)
     stats = by_owner(stats).reshape(16, 3 * own_rows)
     stats = lax.all_to_all(stats, ("z", "h", "k"), split_axis=0, concat_axis=0, tiled=True)
     stats = stats.reshape(16, 3, own_rows)
@@ -298,8 +288,8 @@
 
 
 def on_device(hidden, tokens, old_weight, new_weight):
-    na, nb = first_moves(new_weight)
-    return log_probs(hidden, tokens, old_weight), move_weight(na, nb)
+    n = first_moves(new_weight)
+    return log_probs(hidden, tokens, old_weight), move_weight(n)
 
 
 def solution(mesh):

time: 248 us -> 226 us (0.911)
  the two profiles are of different devices: /device:TPU:1 before, /device:TPU:40 now
where the time goes in v3:
time: 226 us
  waiting for transfers between devices  124 us (55%)
  starting transfers between devices  48.7 us (22%)
  Pallas kernels  43 us (19%)
  local copies, waits for them, and re-layouts  8.04 us (4%)
    ppermute x22, waiting for transfers between devices, send(): return lax.ppermute(value, AXES, pairs(move))  124 us
    ppermute x22, starting transfers between devices, send(): return lax.ppermute(value, AXES, pairs(move))  45.3 us
    pallas_call x2, Pallas kernels, row_stats(): pl.pallas_call(stats_kernel, out_shape=jax.ShapeDtypeStruct((3, count), j...  25.6 us
    pallas_call x3, Pallas kernels, lay(): pl.pallas_call(laid(spots), out_shape=jax.ShapeDtypeStruct((4 * CHUNK, 51...  12.2 us
  transfers between devices with their start and end apart: 23, of which 12 were waited for; matrix products, arithmetic and copies ran while one was open for 3% of the time, Pallas kernels for 17%

profile of v3, /device:TPU:40, one launch (start us, length us, event | category | flops | bytes accessed | tf_op | source)
XLA Modules:
  0.0 225.7 jit_solution(13016746902755404151)
XLA Ops:
  4.9 14.0 %collective-permute-done.3.refs_4_ = bf16[64,5120]{1,0:T(8,128)(2,1)S(1)} collective-permute-done((bf16[64,5120]{1,0:T(8,128)(2,1)}, bf16[64,5120]{1,0:T(8,128)(2,1)S(1)}, u32[]{:S(2)}, u32[]{:S(2)}) %collective-permute-start.3) | collective-permute-done | bytes 655392 | tf_op jit(solution)/shard_map/ppermute | solution.py:33
  19.0 4.0 %collective-permute-start.2 = (bf16[64,5120]{1,0:T(8,128)(2,1)}, bf16[64,5120]{1,0:T(8,128)(2,1)S(1)}, u32[]{:S(2)}, u32[]{:S(2)}) collective-permute-start(bf16[64,5120]{1,0:T(8,128)(2,1)} %refs_0_.1), channel_id=1, source_target_pairs={{0,12},{1,13},{2,14},{3,15},{4,0},{5,1},{6,2},{7,3},{8,4},{9,5},{1... | collective-permute-start | bytes 1966088 | tf_op jit(solution)/shard_map/ppermute | solution.py:33
  23.1 13.4 %collective-permute-done.5.refs_7_ = bf16[64,5120]{1,0:T(8,128)(2,1)S(1)} collective-permute-done((bf16[64,5120]{1,0:T(8,128)(2,1)S(1)}, bf16[64,5120]{1,0:T(8,128)(2,1)S(1)}, u32[]{:S(2)}, u32[]{:S(2)}) %collective-permute-start.5) | collective-permute-done | bytes 655392 | tf_op jit(solution)/shard_map/ppermute | solution.py:33
  38.2 12.4 %collective-permute-done.2.refs_3_ = bf16[64,5120]{1,0:T(8,128)(2,1)S(1)} collective-permute-done((bf16[64,5120]{1,0:T(8,128)(2,1)}, bf16[64,5120]{1,0:T(8,128)(2,1)S(1)}, u32[]{:S(2)}, u32[]{:S(2)}) %collective-permute-start.2) | collective-permute-done | bytes 655392 | tf_op jit(solution)/shard_map/ppermute | solution.py:33
  52.2 10.6 %collective-permute-done.6.refs_6_ = bf16[64,5120]{1,0:T(8,128)(2,1)S(1)} collective-permute-done((bf16[64,5120]{1,0:T(8,128)(2,1)S(1)}, bf16[64,5120]{1,0:T(8,128)(2,1)S(1)}, u32[]{:S(2)}, u32[]{:S(2)}) %collective-permute-start.6) | collective-permute-done | bytes 655392 | tf_op jit(solution)/shard_map/ppermute | solution.py:33
  63.9 4.1 %shard_map.59.hidden_ref = bf16[512,5120]{1,0:T(8,128)(2,1)} custom-call(bf16[64,5120]{1,0:T(8,128)(2,1)S(1)} %copy-done.1, bf16[64,5120]{1,0:T(8,128)(2,1)S(1)} %collective-permute-done.refs_1_, bf16[64,5120]{1,0:T(8,128)(2,1)S(1)} %collective-permute-done.1.refs_2_, bf16[64,5120]{1,0:T(8,128)(2,1)S(1)} %collective-permute-done.2.refs_3_, ...), custom_call_target="tpu_custom_call" | custom-call | tf_op jit(solution)/shard_map/pallas_call | solution.py:238
  68.8 9.2 %collective-permute-done.8.got_ref = bf16[320,1152]{1,0:T(8,128)(2,1)S(1)} collective-permute-done((bf16[320,1152]{1,0:T(8,128)(2,1)S(1)}, bf16[320,1152]{1,0:T(8,128)(2,1)S(1)}, u32[]{:S(2)}, u32[]{:S(2)}) %collective-permute-start.8) | collective-permute-done | bytes 737312 | tf_op jit(solution)/shard_map/ppermute | solution.py:33
  79.1 5.3 %collective-permute-start.9 = (bf16[288,640]{1,0:T(8,128)(2,1)S(1)}, bf16[288,640]{1,0:T(8,128)(2,1)S(1)}, u32[]{:S(2)}, u32[]{:S(2)}) collective-permute-start(bf16[288,640]{1,0:T(8,128)(2,1)S(1)} %get-tuple-element.6), channel_id=1, source_target_pairs={{0,0},{1,1},{2,16},{3,17},{4,32},{5,33},{6,48},{7,49},{8,64},{9,65... | collective-permute-start | bytes 1105928 | tf_op jit(solution)/shard_map/ppermute | solution.py:33
  84.4 5.6 %collective-permute-start.10 = (bf16[288,640]{1,0:T(8,128)(2,1)S(1)}, bf16[288,640]{1,0:T(8,128)(2,1)S(1)}, u32[]{:S(2)}, u32[]{:S(2)}) collective-permute-start(bf16[288,640]{1,0:T(8,128)(2,1)S(1)} %get-tuple-element.7), channel_id=1, source_target_pairs={{0,32},{1,33},{2,48},{3,49},{4,64},{5,65},{6,80},{7,81},{8,96},{9,... | collective-permute-start | bytes 1105928 | tf_op jit(solution)/shard_map/ppermute | solution.py:33
  90.1 5.7 %collective-permute-start.11 = (bf16[288,640]{1,0:T(8,128)(2,1)S(1)}, bf16[288,640]{1,0:T(8,128)(2,1)S(1)}, u32[]{:S(2)}, u32[]{:S(2)}) collective-permute-start(bf16[288,640]{1,0:T(8,128)(2,1)S(1)} %get-tuple-element.8), channel_id=1, source_target_pairs={{0,64},{1,65},{2,80},{3,81},{4,96},{5,97},{6,112},{7,113},{8,0},{9... | collective-permute-start | bytes 1105928 | tf_op jit(solution)/shard_map/ppermute | solution.py:33
  95.8 3.9 %collective-permute-start.12 = (bf16[288,640]{1,0:T(8,128)(2,1)S(1)}, bf16[288,640]{1,0:T(8,128)(2,1)S(1)}, u32[]{:S(2)}, u32[]{:S(2)}) collective-permute-start(bf16[288,640]{1,0:T(8,128)(2,1)S(1)} %get-tuple-element.9), channel_id=1, source_target_pairs={{0,96},{1,97},{2,112},{3,113},{4,0},{5,1},{6,16},{7,17},{8,32},{9,... | collective-permute-start | bytes 1105928 | tf_op jit(solution)/shard_map/ppermute | solution.py:33
  99.7 8.7 %collective-permute-done.10 = bf16[288,640]{1,0:T(8,128)(2,1)S(1)} collective-permute-done((bf16[288,640]{1,0:T(8,128)(2,1)S(1)}, bf16[288,640]{1,0:T(8,128)(2,1)S(1)}, u32[]{:S(2)}, u32[]{:S(2)}) %collective-permute-start.10) | collective-permute-done | bytes 368672 | tf_op jit(solution)/shard_map/ppermute | solution.py:33
  108.4 4.6 %collective-permute-done.11 = bf16[288,640]{1,0:T(8,128)(2,1)S(1)} collective-permute-done((bf16[288,640]{1,0:T(8,128)(2,1)S(1)}, bf16[288,640]{1,0:T(8,128)(2,1)S(1)}, u32[]{:S(2)}, u32[]{:S(2)}) %collective-permute-start.11) | collective-permute-done | bytes 368672 | tf_op jit(solution)/shard_map/ppermute | solution.py:33
  113.1 9.9 %collective-permute-done.12 = bf16[288,640]{1,0:T(8,128)(2,1)S(1)} collective-permute-done((bf16[288,640]{1,0:T(8,128)(2,1)S(1)}, bf16[288,640]{1,0:T(8,128)(2,1)S(1)}, u32[]{:S(2)}, u32[]{:S(2)}) %collective-permute-start.12) | collective-permute-done | bytes 368672 | tf_op jit(solution)/shard_map/ppermute | solution.py:33
  123.2 5.9 %collective-permute-start.16 = (bf16[4,288,640]{2,1,0:T(8,128)(2,1)S(1)}, bf16[4,288,640]{2,1,0:T(8,128)(2,1)S(1)}, u32[]{:S(2)}, u32[]{:S(2)}) collective-permute-start(bf16[4,288,640]{2,1,0:T(8,128)(2,1)S(1)} %pad_maximum_fusion.refs_0_), channel_id=1, source_target_pairs={{0,32},{1,33},{2,34},{3,35},{4,36},{5,37},{6,38},{7,39},{8,40},{9,... | collective-permute-start | bytes 4423688 | tf_op jit(solution)/shard_map/ppermute | solution.py:33
  129.2 31.5 %collective-permute-done.16.refs_1_ = bf16[4,288,640]{2,1,0:T(8,128)(2,1)S(1)} collective-permute-done((bf16[4,288,640]{2,1,0:T(8,128)(2,1)S(1)}, bf16[4,288,640]{2,1,0:T(8,128)(2,1)S(1)}, u32[]{:S(2)}, u32[]{:S(2)}) %collective-permute-start.16) | collective-permute-done | bytes 1474592 | tf_op jit(solution)/shard_map/ppermute | solution.py:33
  161.8 2.5 %collective-permute-start.17 = (bf16[2,288,640]{2,1,0:T(8,128)(2,1)}, bf16[2,288,640]{2,1,0:T(8,128)(2,1)}, u32[]{:S(2)}, u32[]{:S(2)}) collective-permute-start(bf16[2,288,640]{2,1,0:T(8,128)(2,1)} %slice.34), channel_id=1, source_target_pairs={{0,32},{1,33},{2,34},{3,35},{4,36},{5,37},{6,38},{7,39},{8,40},{9,... | collective-permute-start | bytes 2211848 | tf_op jit(solution)/shard_map/ppermute | solution.py:33
  171.8 12.8 %shard_map.60 = f32[3,512]{1,0:T(4,128)} custom-call(s32[1,512]{1,0:T(1,128)} %reshape_squeeze.6.ids_ref, bf16[512,5120]{1,0:T(8,128)(2,1)} %shard_map.59.hidden_ref, bf16[1152,5120]{1,0:T(8,128)(2,1)} %weight_ref.3), custom_call_target="tpu_custom_call" | custom-call | tf_op jit(solution)/shard_map/pallas_call | solution.py:205
  187.5 12.8 %shard_map.61 = f32[3,512]{1,0:T(4,128)} custom-call(s32[1,512]{1,0:T(1,128)} %reshape_squeeze.7.ids_ref, bf16[512,5120]{1,0:T(8,128)(2,1)} %collective-permute-done.7.hidden_ref, bf16[1152,5120]{1,0:T(8,128)(2,1)} %weight_ref.3), custom_call_target="tpu_custom_call" | custom-call | tf_op jit(solution)/shard_map/pallas_call | solution.py:205
  201.9 3.4 %all-to-all-start = ((f32[16,1,192]{2,1,0:T(1,128)}), f32[16,1,192]{2,1,0:T(1,128)S(1)}, u32[]{:S(2)}, u32[]{:S(2)}) async-start(f32[16,1,192]{2,1,0:T(1,128)} %all_to_all.8), calls=%async_computation | async-start | bytes 32768 | tf_op jit(solution)/shard_map/all_to_all | solution.py:282
  205.3 5.3 %shard_map.62.refs_4_ = bf16[1152,5120]{1,0:T(8,128)(2,1)} custom-call(s32[3]{0:T(128)S(1)} %pad_add_fusion.where_ref, bf16[4,288,640]{2,1,0:T(8,128)(2,1)S(1)} %pad_maximum_fusion.refs_0_, bf16[4,288,640]{2,1,0:T(8,128)(2,1)S(1)} %collective-permute-done.16.refs_1_, bf16[4,288,640]{2,1,0:T(8,128)(2,1)} %collective-permute-done.18.refs_2_, ...), custom_call_target="tpu_custom_call" | custom-call | tf_op jit(solution)/shard_map/pallas_call | solution.py:126
  210.7 7.4 %collective-permute-done.21.refs_3_ = bf16[2,288,640]{2,1,0:T(8,128)(2,1)} collective-permute-done((bf16[2,288,640]{2,1,0:T(8,128)(2,1)}, bf16[2,288,640]{2,1,0:T(8,128)(2,1)}, u32[]{:S(2)}, u32[]{:S(2)}) %collective-permute-start.21) | collective-permute-done | bytes 737312 | tf_op jit(solution)/shard_map/ppermute | solution.py:33
  218.0 3.3 %shard_map.63.refs_2_ = bf16[1152,5120]{1,0:T(8,128)(2,1)} custom-call(s32[3]{0:T(128)S(1)} %pad_add_fusion.where_ref, bf16[2,288,640]{2,1,0:T(8,128)(2,1)} %collective-permute-done.17.refs_0_, bf16[2,288,640]{2,1,0:T(8,128)(2,1)} %collective-permute-done.19.refs_1_, ...), custom_call_target="tpu_custom_call", output_to_operand_aliasing={{}: (5, {})} | custom-call | tf_op jit(solution)/shard_map/pallas_call | solution.py:126
  221.4 3.6 %shard_map.64 = bf16[1152,5120]{1,0:T(8,128)(2,1)} custom-call(s32[3]{0:T(128)S(1)} %pad_add_fusion.where_ref, bf16[4,288,640]{2,1,0:T(8,128)(2,1)} %collective-permute-done.14.refs_0_, bf16[4,288,640]{2,1,0:T(8,128)(2,1)} %collective-permute-done.15.refs_1_, bf16[1152,5120]{1,0:T(8,128)(2,1)} %shard_map.63.refs_2_), custom_call_target="tpu_custom_call", output_to_operand_aliasing={{}: (3, {})} | custom-call | tf_op jit(solution)/shard_map/pallas_call | solution.py:126
  (68 shorter events, 24.7 us)
Async XLA Ops:
  0.6 67.4 %copy-start = (bf16[2304,320]{0,1:T(8,128)(2,1)S(1)}, bf16[2304,320]{0,1:T(8,128)(2,1)}, u32[]{:S(2)}) copy-start(bf16[2304,320]{0,1:T(8,128)(2,1)} %param.7) | copy-start | bytes 4423684
  0.6 18.3 %collective-permute-start.3 = (bf16[64,5120]{1,0:T(8,128)(2,1)}, bf16[64,5120]{1,0:T(8,128)(2,1)S(1)}, u32[]{:S(2)}, u32[]{:S(2)}) collective-permute-start(bf16[64,5120]{1,0:T(8,128)(2,1)} %refs_0_.1), channel_id=1, source_target_pairs={{0,2},{1,3},{2,0},{3,1},{4,6},{5,7},{6,4},{7,5},{8,10},{9,11},{10,... | collective-permute-start | bytes 1966088 | tf_op jit(solution)/shard_map/ppermute | solution.py:33
  3.0 20.0 %collective-permute-start = (bf16[64,5120]{1,0:T(8,128)(2,1)}, bf16[64,5120]{1,0:T(8,128)(2,1)S(1)}, u32[]{:S(2)}, u32[]{:S(2)}) collective-permute-start(bf16[64,5120]{1,0:T(8,128)(2,1)} %refs_0_.1), channel_id=1, source_target_pairs={{0,4},{1,5},{2,6},{3,7},{4,8},{5,9},{6,10},{7,11},{8,12},{9,13},{1... | collective-permute-start | bytes 1966088 | tf_op jit(solution)/shard_map/ppermute | solution.py:33
  18.9 17.6 %collective-permute-start.5 = (bf16[64,5120]{1,0:T(8,128)(2,1)S(1)}, bf16[64,5120]{1,0:T(8,128)(2,1)S(1)}, u32[]{:S(2)}, u32[]{:S(2)}) collective-permute-start(bf16[64,5120]{1,0:T(8,128)(2,1)S(1)} %collective-permute-done.3.refs_4_), channel_id=1, source_target_pairs={{0,12},{1,13},{2,14},{3,15},{4,0},{5,1},{6,2},{7,3},{8,4},{9,5},{1... | collective-permute-start | bytes 1966088 | tf_op jit(solution)/shard_map/ppermute | solution.py:33
  19.0 31.5 %collective-permute-start.2 = (bf16[64,5120]{1,0:T(8,128)(2,1)}, bf16[64,5120]{1,0:T(8,128)(2,1)S(1)}, u32[]{:S(2)}, u32[]{:S(2)}) collective-permute-start(bf16[64,5120]{1,0:T(8,128)(2,1)} %refs_0_.1), channel_id=1, source_target_pairs={{0,12},{1,13},{2,14},{3,15},{4,0},{5,1},{6,2},{7,3},{8,4},{9,5},{1... | collective-permute-start | bytes 1966088 | tf_op jit(solution)/shard_map/ppermute | solution.py:33
  23.1 27.5 %collective-permute-start.4 = (bf16[64,5120]{1,0:T(8,128)(2,1)S(1)}, bf16[64,5120]{1,0:T(8,128)(2,1)S(1)}, u32[]{:S(2)}, u32[]{:S(2)}) collective-permute-start(bf16[64,5120]{1,0:T(8,128)(2,1)S(1)} %collective-permute-done.3.refs_4_), channel_id=1, source_target_pairs={{0,4},{1,5},{2,6},{3,7},{4,8},{5,9},{6,10},{7,11},{8,12},{9,13},{1... | collective-permute-start | bytes 1966088 | tf_op jit(solution)/shard_map/ppermute | solution.py:33
  23.1 29.1 %collective-permute-start.1 = (bf16[64,5120]{1,0:T(8,128)(2,1)S(1)}, bf16[64,5120]{1,0:T(8,128)(2,1)S(1)}, u32[]{:S(2)}, u32[]{:S(2)}) collective-permute-start(bf16[64,5120]{1,0:T(8,128)(2,1)S(1)} %collective-permute-done.refs_1_), channel_id=1, source_target_pairs={{0,4},{1,5},{2,6},{3,7},{4,8},{5,9},{6,10},{7,11},{8,12},{9,13},{1... | collective-permute-start | bytes 1966088 | tf_op jit(solution)/shard_map/ppermute | solution.py:33
  36.5 26.3 %collective-permute-start.6 = (bf16[64,5120]{1,0:T(8,128)(2,1)S(1)}, bf16[64,5120]{1,0:T(8,128)(2,1)S(1)}, u32[]{:S(2)}, u32[]{:S(2)}) collective-permute-start(bf16[64,5120]{1,0:T(8,128)(2,1)S(1)} %collective-permute-done.5.refs_7_), channel_id=1, source_target_pairs={{0,12},{1,13},{2,14},{3,15},{4,0},{5,1},{6,2},{7,3},{8,4},{9,5},{1... | collective-permute-start | bytes 1966088 | tf_op jit(solution)/shard_map/ppermute | solution.py:33
  68.0 119.5 %collective-permute-start.7 = (bf16[512,5120]{1,0:T(8,128)(2,1)}, bf16[512,5120]{1,0:T(8,128)(2,1)}, u32[]{:S(2)}, u32[]{:S(2)}) collective-permute-start(bf16[512,5120]{1,0:T(8,128)(2,1)} %shard_map.59.hidden_ref), channel_id=1, source_target_pairs={{0,1},{1,0},{2,3},{3,2},{4,5},{5,4},{6,7},{7,6},{8,9},{9,8},{10,11... | collective-permute-start | bytes 15728648 | tf_op jit(solution)/shard_map/ppermute | solution.py:33
  68.1 9.8 %collective-permute-start.8 = (bf16[320,1152]{1,0:T(8,128)(2,1)S(1)}, bf16[320,1152]{1,0:T(8,128)(2,1)S(1)}, u32[]{:S(2)}, u32[]{:S(2)}) collective-permute-start(bf16[320,1152]{1,0:T(8,128)(2,1)S(1)} %dynamic-slice_bitcast_fusion), channel_id=1, source_target_pairs={{0,1},{1,0},{2,3},{3,2},{4,5},{5,4},{6,7},{7,6},{8,9},{9,8},{10,11... | collective-permute-start | bytes 2211848 | tf_op jit(solution)/shard_map/ppermute | solution.py:33
  79.1 20.6 %collective-permute-start.9 = (bf16[288,640]{1,0:T(8,128)(2,1)S(1)}, bf16[288,640]{1,0:T(8,128)(2,1)S(1)}, u32[]{:S(2)}, u32[]{:S(2)}) collective-permute-start(bf16[288,640]{1,0:T(8,128)(2,1)S(1)} %get-tuple-element.6), channel_id=1, source_target_pairs={{0,0},{1,1},{2,16},{3,17},{4,32},{5,33},{6,48},{7,49},{8,64},{9,65... | collective-permute-start | bytes 1105928 | tf_op jit(solution)/shard_map/ppermute | solution.py:33
  84.4 24.0 %collective-permute-start.10 = (bf16[288,640]{1,0:T(8,128)(2,1)S(1)}, bf16[288,640]{1,0:T(8,128)(2,1)S(1)}, u32[]{:S(2)}, u32[]{:S(2)}) collective-permute-start(bf16[288,640]{1,0:T(8,128)(2,1)S(1)} %get-tuple-element.7), channel_id=1, source_target_pairs={{0,32},{1,33},{2,48},{3,49},{4,64},{5,65},{6,80},{7,81},{8,96},{9,... | collective-permute-start | bytes 1105928 | tf_op jit(solution)/shard_map/ppermute | solution.py:33
  90.1 23.0 %collective-permute-start.11 = (bf16[288,640]{1,0:T(8,128)(2,1)S(1)}, bf16[288,640]{1,0:T(8,128)(2,1)S(1)}, u32[]{:S(2)}, u32[]{:S(2)}) collective-permute-start(bf16[288,640]{1,0:T(8,128)(2,1)S(1)} %get-tuple-element.8), channel_id=1, source_target_pairs={{0,64},{1,65},{2,80},{3,81},{4,96},{5,97},{6,112},{7,113},{8,0},{9... | collective-permute-start | bytes 1105928 | tf_op jit(solution)/shard_map/ppermute | solution.py:33
  95.8 27.2 %collective-permute-start.12 = (bf16[288,640]{1,0:T(8,128)(2,1)S(1)}, bf16[288,640]{1,0:T(8,128)(2,1)S(1)}, u32[]{:S(2)}, u32[]{:S(2)}) collective-permute-start(bf16[288,640]{1,0:T(8,128)(2,1)S(1)} %get-tuple-element.9), channel_id=1, source_target_pairs={{0,96},{1,97},{2,112},{3,113},{4,0},{5,1},{6,16},{7,17},{8,32},{9,... | collective-permute-start | bytes 1105928 | tf_op jit(solution)/shard_map/ppermute | solution.py:33
  123.2 37.6 %collective-permute-start.16 = (bf16[4,288,640]{2,1,0:T(8,128)(2,1)S(1)}, bf16[4,288,640]{2,1,0:T(8,128)(2,1)S(1)}, u32[]{:S(2)}, u32[]{:S(2)}) collective-permute-start(bf16[4,288,640]{2,1,0:T(8,128)(2,1)S(1)} %pad_maximum_fusion.refs_0_), channel_id=1, source_target_pairs={{0,32},{1,33},{2,34},{3,35},{4,36},{5,37},{6,38},{7,39},{8,40},{9,... | collective-permute-start | bytes 4423688 | tf_op jit(solution)/shard_map/ppermute | solution.py:33
  129.1 35.1 %collective-permute-start.18 = (bf16[4,288,640]{2,1,0:T(8,128)(2,1)S(1)}, bf16[4,288,640]{2,1,0:T(8,128)(2,1)}, u32[]{:S(2)}, u32[]{:S(2)}) collective-permute-start(bf16[4,288,640]{2,1,0:T(8,128)(2,1)S(1)} %pad_maximum_fusion.refs_0_), channel_id=1, source_target_pairs={{0,96},{1,97},{2,98},{3,99},{4,100},{5,101},{6,102},{7,103},{8,104... | collective-permute-start | bytes 4423688 | tf_op jit(solution)/shard_map/ppermute | solution.py:33
  129.1 38.0 %collective-permute-start.13 = (bf16[4,288,640]{2,1,0:T(8,128)(2,1)S(1)}, bf16[4,288,640]{2,1,0:T(8,128)(2,1)}, u32[]{:S(2)}, u32[]{:S(2)}) collective-permute-start(bf16[4,288,640]{2,1,0:T(8,128)(2,1)S(1)} %pad_maximum_fusion.refs_0_), channel_id=1, source_target_pairs={{0,16},{1,17},{2,18},{3,19},{4,20},{5,21},{6,22},{7,23},{8,24},{9,... | collective-permute-start | bytes 4423688 | tf_op jit(solution)/shard_map/ppermute | solution.py:33
  161.8 23.6 %collective-permute-start.17 = (bf16[2,288,640]{2,1,0:T(8,128)(2,1)}, bf16[2,288,640]{2,1,0:T(8,128)(2,1)}, u32[]{:S(2)}, u32[]{:S(2)}) collective-permute-start(bf16[2,288,640]{2,1,0:T(8,128)(2,1)} %slice.34), channel_id=1, source_target_pairs={{0,32},{1,33},{2,34},{3,35},{4,36},{5,37},{6,38},{7,39},{8,40},{9,... | collective-permute-start | bytes 2211848 | tf_op jit(solution)/shard_map/ppermute | solution.py:33
  166.3 19.7 %collective-permute-start.19 = (bf16[2,288,640]{2,1,0:T(8,128)(2,1)}, bf16[2,288,640]{2,1,0:T(8,128)(2,1)}, u32[]{:S(2)}, u32[]{:S(2)}) collective-permute-start(bf16[2,288,640]{2,1,0:T(8,128)(2,1)} %slice.35), channel_id=1, source_target_pairs={{0,96},{1,97},{2,98},{3,99},{4,100},{5,101},{6,102},{7,103},{8,104... | collective-permute-start | bytes 2211848 | tf_op jit(solution)/shard_map/ppermute | solution.py:33
  167.1 54.3 %collective-permute-start.14 = (bf16[4,288,640]{2,1,0:T(8,128)(2,1)}, bf16[4,288,640]{2,1,0:T(8,128)(2,1)}, u32[]{:S(2)}, u32[]{:S(2)}) collective-permute-start(bf16[4,288,640]{2,1,0:T(8,128)(2,1)} %collective-permute-done.13.refs_3_), channel_id=1, source_target_pairs={{0,32},{1,33},{2,34},{3,35},{4,36},{5,37},{6,38},{7,39},{8,40},{9,... | collective-permute-start | bytes 4423688 | tf_op jit(solution)/shard_map/ppermute | solution.py:33
  168.4 53.0 %collective-permute-start.15 = (bf16[4,288,640]{2,1,0:T(8,128)(2,1)}, bf16[4,288,640]{2,1,0:T(8,128)(2,1)}, u32[]{:S(2)}, u32[]{:S(2)}) collective-permute-start(bf16[4,288,640]{2,1,0:T(8,128)(2,1)} %collective-permute-done.13.refs_3_), channel_id=1, source_target_pairs={{0,96},{1,97},{2,98},{3,99},{4,100},{5,101},{6,102},{7,103},{8,104... | collective-permute-start | bytes 4423688 | tf_op jit(solution)/shard_map/ppermute | solution.py:33
  185.4 25.3 %collective-permute-start.20 = (bf16[2,288,640]{2,1,0:T(8,128)(2,1)}, bf16[2,288,640]{2,1,0:T(8,128)(2,1)}, u32[]{:S(2)}, u32[]{:S(2)}) collective-permute-start(bf16[2,288,640]{2,1,0:T(8,128)(2,1)} %collective-permute-done.17.refs_0_), channel_id=1, source_target_pairs={{0,16},{1,17},{2,18},{3,19},{4,20},{5,21},{6,22},{7,23},{8,24},{9,... | collective-permute-start | bytes 2211848 | tf_op jit(solution)/shard_map/ppermute | solution.py:33
  186.0 32.0 %collective-permute-start.21 = (bf16[2,288,640]{2,1,0:T(8,128)(2,1)}, bf16[2,288,640]{2,1,0:T(8,128)(2,1)}, u32[]{:S(2)}, u32[]{:S(2)}) collective-permute-start(bf16[2,288,640]{2,1,0:T(8,128)(2,1)} %collective-permute-done.19.refs_1_), channel_id=1, source_target_pairs={{0,16},{1,17},{2,18},{3,19},{4,20},{5,21},{6,22},{7,23},{8,24},{9,... | collective-permute-start | bytes 2211848 | tf_op jit(solution)/shard_map/ppermute | solution.py:33
  201.9 23.1 %all-to-all-start = ((f32[16,1,192]{2,1,0:T(1,128)}), f32[16,1,192]{2,1,0:T(1,128)S(1)}, u32[]{:S(2)}, u32[]{:S(2)}) async-start(f32[16,1,192]{2,1,0:T(1,128)} %all_to_all.8), calls=%async_computation | async-start | bytes 32768 | tf_op jit(solution)/shard_map/all_to_all | solution.py:282
  (2 other events, 7.2 us)
